TPU v7x, 8 devices: a whole 2x2x1 slice. The times are simulated.
8 devices in a mesh: dp: 2 (over z, y), tp: 4 (over x, core).
Axes of the slice: x: 2, y: 2, z: 1, core: 2. Of those that a mesh axis runs over, the one named last changes fastest.
Arguments:
- hidden: bfloat16 [2, 256, 3584], P('dp', 'tp'), parts along dimension 0
- positions: int32 [2, 256], P('dp'), parts along dimension 0
- gain_attn: bfloat16 [3584], replicated
- w_q: bfloat16 [3584, 3584], P(None, 'tp')
- b_q: bfloat16 [3584], P('tp')
- w_k: bfloat16 [3584, 512], P(None, 'tp')
- b_k: bfloat16 [512], P('tp')
- w_v: bfloat16 [3584, 512], P(None, 'tp')
- b_v: bfloat16 [512], P('tp')
- w_o: bfloat16 [3584, 3584], P('tp')
- gain_mlp: bfloat16 [3584], replicated
- w_gate: bfloat16 [3584, 18944], P(None, 'tp')
- w_up: bfloat16 [3584, 18944], P(None, 'tp')
- w_down: bfloat16 [18944, 3584], P('tp')
Outputs:
- output 1: bfloat16 [2, 256, 3584], P('dp', 'tp'), parts along dimension 0
- output 2: bfloat16 [2, 256, 4, 128], P('dp', None, 'tp'), parts along dimension 0
- output 3: bfloat16 [2, 256, 4, 128], P('dp', None, 'tp'), parts along dimension 0
There are 2 independent parts. A program takes and returns all parts, laid end to end along the dimension named above; an argument that names none is the same for every part.
All inputs are finite; a program needn't handle non-finite values.
Results may differ from a plain program's by a relative error of at most 0.0126876.
Values are sent between devices in bfloat16 or wider.
A program may use at most 1 GiB of HBM per device.

v0:
```python
import jax
import jax.numpy as jnp
from jax import lax
from jax.sharding import PartitionSpec as P, NamedSharding

HEAD_DIM = 128
ROPE_THETA = 1000000.0
NORM_EPS = 1e-6


def rms_norm(values, gain):
    values_f32 = values.astype(jnp.float32)
    inv_rms = lax.rsqrt(jnp.mean(values_f32 * values_f32, axis=-1, keepdims=True) + NORM_EPS)
    return (values_f32 * inv_rms * gain.astype(jnp.float32)).astype(jnp.bfloat16)


def rotary(values, positions):
    half_dim = HEAD_DIM // 2
    inv_freq = ROPE_THETA ** (-jnp.arange(half_dim, dtype=jnp.float32) / half_dim)
    angles = positions.astype(jnp.float32)[:, :, None] * inv_freq
    angles = angles.reshape(angles.shape[:2] + (1,) * (values.ndim - 3) + (half_dim,))
    cosine = jnp.cos(angles)
    sine = jnp.sin(angles)
    first = values[..., :half_dim]
    second = values[..., half_dim:]
    return jnp.concatenate([first * cosine - second * sine, second * cosine + first * sine], axis=-1)


def project(normed, weight, bias):
    return jnp.einsum('btd,df->btf', normed, weight, preferred_element_type=jnp.float32) + bias.astype(jnp.float32)


def attention(query, key_heads, value_heads):
    seq_len = query.shape[1]
    causal = jnp.arange(seq_len)[:, None] >= jnp.arange(seq_len)[None, :]
    scores = jnp.einsum('btkgd,bskd->bkgts', query, key_heads, preferred_element_type=jnp.float32) * (HEAD_DIM ** -0.5)
    scores = jnp.where(causal, scores, -1e30)
    attn_probs = jax.nn.softmax(scores, axis=-1).astype(jnp.bfloat16)
    attn_out = jnp.einsum('bkgts,bskd->btkgd', attn_probs, value_heads, preferred_element_type=jnp.float32)
    return attn_out.astype(jnp.bfloat16).reshape(query.shape[0], seq_len, -1)


def solution(mesh):
    def local_layer(hidden, positions, gain_attn, w_q, b_q, w_k, b_k, w_v, b_v, w_o, gain_mlp, w_gate, w_up, w_down):
        batch = hidden.shape[0]
        seq_len = positions.shape[1]
        kv_local = w_k.shape[1] // HEAD_DIM
        group = w_q.shape[1] // w_k.shape[1]
        normed = rms_norm(hidden, gain_attn)
        normed_all = lax.all_gather(normed, 'tp', axis=1, tiled=True)
        query = project(normed_all, w_q, b_q).reshape(batch, seq_len, kv_local, group, HEAD_DIM)
        query = rotary(query, positions).astype(jnp.bfloat16)
        key_proj = project(normed_all, w_k, b_k).reshape(batch, seq_len, kv_local, HEAD_DIM)
        k_cache = rotary(key_proj, positions).astype(jnp.bfloat16)
        v_cache = project(normed_all, w_v, b_v).reshape(batch, seq_len, kv_local, HEAD_DIM).astype(jnp.bfloat16)
        attn_out = attention(query, k_cache, v_cache)
        attn_part = jnp.einsum('btf,fd->btd', attn_out, w_o, preferred_element_type=jnp.float32).astype(jnp.bfloat16)
        attn_sum = lax.psum_scatter(attn_part, 'tp', scatter_dimension=1, tiled=True)
        hidden_mid = (hidden.astype(jnp.float32) + attn_sum.astype(jnp.float32)).astype(jnp.bfloat16)
        normed_mid = rms_norm(hidden_mid, gain_mlp)
        normed_mid_all = lax.all_gather(normed_mid, 'tp', axis=1, tiled=True)
        gate = jnp.einsum('btd,df->btf', normed_mid_all, w_gate, preferred_element_type=jnp.float32)
        up_proj = jnp.einsum('btd,df->btf', normed_mid_all, w_up, preferred_element_type=jnp.float32)
        activation = (jax.nn.silu(gate) * up_proj).astype(jnp.bfloat16)
        down_part = jnp.einsum('btf,fd->btd', activation, w_down, preferred_element_type=jnp.float32).astype(jnp.bfloat16)
        down_sum = lax.psum_scatter(down_part, 'tp', scatter_dimension=1, tiled=True)
        hidden_out = (hidden_mid.astype(jnp.float32) + down_sum.astype(jnp.float32)).astype(jnp.bfloat16)
        return hidden_out, k_cache, v_cache

    token_rows = P('dp', 'tp', None)
    col_split = P(None, 'tp')
    row_split = P('tp', None)
    vec_split = P('tp')
    replicated = P(None)
    cache_spec = P('dp', None, 'tp', None)
    in_specs = (token_rows, P('dp', None), replicated, col_split, vec_split, col_split, vec_split, col_split, vec_split, row_split, replicated, col_split, col_split, row_split)
    out_specs = (token_rows, cache_spec, cache_spec)
    return jax.shard_map(local_layer, mesh=mesh, in_specs=in_specs, out_specs=out_specs, check_vma=False)
```

profile of v0, /device:TPU:0, one launch (start us, length us, event | category | flops | bytes accessed | tf_op | source)
XLA Modules:
  0.0 185.9 jit_solution(2685334729954995211)
XLA Ops:
  7.2 0.0 copy-start
  7.2 0.0 all-gather.3.cloned.1.call-start
  7.3 1.3 fusion.37
  8.6 0.7 convert_element_type.101
  9.3 2.0 %fusion.39 = bf16[1,64,3584]{2,1,0:T(8,128)(2,1)} fusion(bf16[1,64,3584]{2,1,0:T(8,128)(2,1)} %param.14, f32[3584]{0:T(1024)S(1)} %convert_element_type.101, f32[64]{0:T(128)S(1)} %add_rsqrt_fusion.1), kind=kLoop, calls=%fused_computation.40 | loop fusion | flops 917504 | bytes 932096 | tf_op jit(solution)/shard_map/convert_element_type | solution.py:14
  11.2 0.0 all-gather.3.cloned.1.call-update
  11.3 0.0 reduce-scatter.3.cloned.1.call-start
  11.3 0.0 copy-done.10
  11.4 0.7 iota_compare_fusion
  12.1 0.5 multiply_cosine_fusion
  12.6 19.7 %all-gather.3.cloned.1.call-done = bf16[1,256,3584]{2,1,0:T(8,128)(2,1)} async-done(((bf16[1,64,3584]{2,1,0:T(8,128)(2,1)}), bf16[1,256,3584]{2,1,0:T(8,128)(2,1)}) %all-gather.3.cloned.1.call-update) | async-done | bytes 1835024 | tf_op jit(solution)/shard_map/all_gather | solution.py:50
  32.3 0.0 copy-done
  32.3 2.4 %fusion.31 = f32[1,256,1,128]{1,3,2,0:T(8,128)S(1)} fusion(bf16[3584,128]{1,0:T(8,128)(2,1)S(1)} %copy-done, bf16[1,256,3584]{2,1,0:T(8,128)(2,1)} %all-gather.3.cloned.1.call-done, f32[128]{0:T(128)S(1)} %convert_element_type.105), kind=kOutput, calls=%fused_computation.36 | convolution fusion | flops 234913792 | bytes 2884096 | tf_op jit(solution)/shard_map/btd,df->btf/dot_general | solution.py:30
  34.7 0.3 fusion.56
  35.1 5.8 %fusion.22 = f32[256,896]{1,0:T(8,128)} fusion(bf16[3584,896]{1,0:T(8,128)(2,1)} %param.17, bf16[1,256,3584]{2,1,0:T(8,128)(2,1)S(1)} %copy-done.3, f32[896]{0:T(1024)S(1)} %convert_element_type.108), kind=kOutput, calls=%fused_computation.32 | convolution fusion | flops 1644396544 | bytes 9178624 | tf_op jit(solution)/shard_map/btd,df->btf/dot_general | solution.py:30
  40.9 1.5 copy.23
  42.4 0.9 fusion.64
  43.2 1.3 copy.36
  44.5 1.2 copy.35
  45.8 1.5 fusion.46
  47.2 0.0 copy-start.5
  47.2 0.0 slice-start
  47.3 0.6 fusion.65
  47.9 0.3 fusion.21
  48.1 0.3 copy-done.5
  48.4 0.6 fusion.34
  49.0 0.0 copy-start.7
  49.0 0.5 convolution_convert_fusion.1
  49.5 0.1 copy-done.7
  49.7 0.0 slice-done
  49.7 0.9 slice-done.1
  50.6 3.4 %fusion.3 = bf16[1,256,3584]{2,1,0:T(8,128)(2,1)} fusion(bf16[256,896]{0,1:T(8,128)(2,1)S(1)} %bitcast.69, bf16[896,3584]{1,0:T(8,128)(2,1)S(1)} %bitcast.67), kind=kOutput, calls=%fused_computation.5 | convolution fusion | flops 1645084672 | bytes 8716288 | tf_op jit(solution)/shard_map/btf,fd->btd/dot_general | solution.py:57
  54.1 0.0 reduce-scatter.3.cloned.1.call-update
  54.1 0.0 all-gather.5.cloned.1.call-start
  54.1 0.6 copy-done.8
  54.8 23.4 %reduce-scatter.3.cloned.1.call-done = bf16[1,64,3584]{2,1,0:T(8,128)(2,1)} async-done(((bf16[1,256,3584]{2,1,0:T(8,128)(2,1)}), bf16[1,64,3584]{2,1,0:T(8,128)(2,1)}) %reduce-scatter.3.cloned.1.call-update) | async-done | bytes 458768 | tf_op jit(solution)/shard_map/reduce_scatter | solution.py:58
  78.2 1.3 fusion.41
  79.5 2.0 %fusion.43 = bf16[1,64,3584]{2,1,0:T(8,128)(2,1)} fusion(f32[3584]{0:T(1024)S(1)} %convert_element_type.118, f32[64]{0:T(128)S(1)} %add_rsqrt_fusion, bf16[1,64,3584]{2,1,0:T(8,128)(2,1)} %reduce-scatter.3.cloned.1.call-done, bf16[1,64,3584]{2,1,0:T(8,128)(2,1)S(1)} %copy-done.2), kind=kLoop, calls=%fused_computation.44 | loop fusion | flops 1835008 | bytes 1390848 | tf_op jit(solution)/shard_map/convert_element_type | solution.py:14
  81.4 0.0 all-gather.5.cloned.1.call-update
  81.5 0.2 reduce-scatter.5.cloned.1.call-start
  81.7 18.0 %all-gather.5.cloned.1.call-done = bf16[1,256,3584]{2,1,0:T(8,128)(2,1)} async-done(((bf16[1,64,3584]{2,1,0:T(8,128)(2,1)}), bf16[1,256,3584]{2,1,0:T(8,128)(2,1)}) %all-gather.5.cloned.1.call-update) | async-done | bytes 1835024 | tf_op jit(solution)/shard_map/all_gather | solution.py:61
  99.7 22.4 %fusion.13 = f32[256,4736]{1,0:T(8,128)} fusion(bf16[3584,4736]{1,0:T(8,128)(2,1)} %param.25, bf16[1,256,3584]{2,1,0:T(8,128)(2,1)} %all-gather.5.cloned.1.call-done), kind=kOutput, calls=%fused_computation.15 | convolution fusion | flops 8690597888 | bytes 40632320 | tf_op jit(solution)/shard_map/btd,df->btf/dot_general | solution.py:62
  122.1 31.2 %fusion.4 = bf16[1,256,3584]{2,1,0:T(8,128)(2,1)} fusion(bf16[4736,3584]{1,0:T(8,128)(2,1)} %param.27, bf16[3584,4736]{1,0:T(8,128)(2,1)} %param.26, f32[256,4736]{1,0:T(8,128)} %fusion.13, bf16[1,256,3584]{2,1,0:T(8,128)(2,1)S(1)} %copy-done.11), kind=kOutput, calls=%fused_computation.6 | convolution fusion | flops 17389387776 | bytes 76414976 | tf_op jit(solution)/shard_map/btf,fd->btd/dot_general | solution.py:65
  153.3 0.0 reduce-scatter.5.cloned.1.call-update
  153.3 0.7 copy.29
  154.1 23.3 %reduce-scatter.5.cloned.1.call-done = bf16[1,64,3584]{2,1,0:T(8,128)(2,1)} async-done(((bf16[1,256,3584]{2,1,0:T(8,128)(2,1)}), bf16[1,64,3584]{2,1,0:T(8,128)(2,1)}) %reduce-scatter.5.cloned.1.call-update) | async-done | bytes 458768 | tf_op jit(solution)/shard_map/reduce_scatter | solution.py:66
  177.4 0.0 copy-done.4
  177.4 2.0 %fusion.44 = bf16[1,64,3584]{2,1,0:T(8,128)(2,1)} fusion(bf16[1,64,3584]{2,1,0:T(8,128)(2,1)} %reduce-scatter.5.cloned.1.call-done, bf16[1,64,3584]{2,1,0:T(8,128)(2,1)S(1)} %copy-done.4, bf16[1,64,3584]{2,1,0:T(8,128)(2,1)S(1)} %copy-done.2), kind=kLoop, calls=%fused_computation.45 | loop fusion | flops 1835008 | bytes 1835008 | tf_op jit(solution)/shard_map/convert_element_type | solution.py:67
  (30 shorter events, 0.1 us)
Async XLA Ops:
  7.2 25.2 %copy-start = (bf16[3584,128]{1,0:T(8,128)(2,1)S(1)}, bf16[3584,128]{1,0:T(8,128)(2,1)}, u32[]{:S(2)}) copy-start(bf16[3584,128]{1,0:T(8,128)(2,1)} %param.19) | copy-start | bytes 2752516
  7.2 4.1 %copy-start.12 = (bf16[128]{0:T(256)(128)(2,1)S(1)}, bf16[128]{0:T(256)(128)(2,1)}, u32[]{:S(2)}) copy-start(bf16[128]{0:T(256)(128)(2,1)} %param.20) | copy-start | bytes 772
  7.2 4.1 %copy-start.13 = (bf16[128]{0:T(256)(128)(2,1)S(1)}, bf16[128]{0:T(256)(128)(2,1)}, u32[]{:S(2)}) copy-start(bf16[128]{0:T(256)(128)(2,1)} %param.22) | copy-start | bytes 772
  7.2 4.1 %copy-start.10 = (s32[1,256]{1,0:T(1,128)S(1)}, s32[1,256]{1,0:T(1,128)}, u32[]{:S(2)}) copy-start(s32[1,256]{1,0:T(1,128)} %param.15) | copy-start | bytes 3076
  7.2 4.2 %copy-start.9 = (bf16[896]{0:T(1024)(128)(2,1)S(1)}, bf16[896]{0:T(1024)(128)(2,1)}, u32[]{:S(2)}) copy-start(bf16[896]{0:T(1024)(128)(2,1)} %param.18) | copy-start | bytes 5380
  7.2 25.1 %all-gather.3.cloned.1.call-start = ((), (), s32[]{:S(2)}) async-start(), calls=%async_computation.2 | async-start | bytes 2293760 | tf_op jit(solution)/shard_map/all_gather | solution.py:50
  11.3 66.9 %reduce-scatter.3.cloned.1.call-start = ((), (), s32[]{:S(2)}) async-start(), calls=%async_computation.3 | async-start | bytes 2293760 | tf_op jit(solution)/shard_map/reduce_scatter | solution.py:58
  32.3 2.7 %copy-start.3 = (bf16[1,256,3584]{2,1,0:T(8,128)(2,1)S(1)}, bf16[1,256,3584]{2,1,0:T(8,128)(2,1)}, u32[]{:S(2)}) copy-start(bf16[1,256,3584]{2,1,0:T(8,128)(2,1)} %all-gather.3.cloned.1.call-done) | copy-start | bytes 5505028
  45.8 1.5 copy-start.6
  47.2 1.2 copy-start.5
  47.2 2.5 %slice-start = ((s8[6422528]{0:T(1024)(128)(4,1)}), s8[4194304]{0:T(1024)(128)(4,1)S(1)}, s32[]{:S(2)}) async-start(s8[6422528]{0:T(1024)(128)(4,1)} %bitcast.66), calls=%async_computation.6 | async-start | bytes 8388608
  48.4 2.2 %slice-start.1 = ((s8[6422528]{0:T(1024)(128)(4,1)}), s8[2228224]{0:T(1024)(128)(4,1)S(1)}, s32[]{:S(2)}) async-start(s8[6422528]{0:T(1024)(128)(4,1)} %bitcast.66), calls=%async_computation.7 | async-start | bytes 4456448
  49.0 0.6 copy-start.7
  54.1 0.7 copy-start.8
  54.1 24.1 %copy-start.2 = (bf16[1,64,3584]{2,1,0:T(8,128)(2,1)S(1)}, bf16[1,64,3584]{2,1,0:T(8,128)(2,1)}, u32[]{:S(2)}) copy-start(bf16[1,64,3584]{2,1,0:T(8,128)(2,1)} %param.14) | copy-start | bytes 1376260
  54.1 45.6 %all-gather.5.cloned.1.call-start = ((), (), s32[]{:S(2)}) async-start(), calls=%async_computation.4 | async-start | bytes 2293760 | tf_op jit(solution)/shard_map/all_gather | solution.py:61
  81.5 95.9 %reduce-scatter.5.cloned.1.call-start = ((), (), s32[]{:S(2)}) async-start(), calls=%async_computation.5 | async-start | bytes 2293760 | tf_op jit(solution)/shard_map/reduce_scatter | solution.py:66
  99.7 22.4 %copy-start.11 = (bf16[1,256,3584]{2,1,0:T(8,128)(2,1)S(1)}, bf16[1,256,3584]{2,1,0:T(8,128)(2,1)}, u32[]{:S(2)}) copy-start(bf16[1,256,3584]{2,1,0:T(8,128)(2,1)} %all-gather.5.cloned.1.call-done) | copy-start | bytes 5505028
  153.3 24.1 %copy-start.4 = (bf16[1,64,3584]{2,1,0:T(8,128)(2,1)S(1)}, bf16[1,64,3584]{2,1,0:T(8,128)(2,1)}, u32[]{:S(2)}) copy-start(bf16[1,64,3584]{2,1,0:T(8,128)(2,1)} %reduce-scatter.3.cloned.1.call-done) | copy-start | bytes 1376260
  153.3 26.1 %copy-start.1 = (bf16[3584,128]{1,0:T(8,128)(2,1)S(1)}, bf16[3584,128]{1,0:T(8,128)(2,1)}, u32[]{:S(2)}) copy-start(bf16[3584,128]{1,0:T(8,128)(2,1)} %param.19) | copy-start | bytes 2752516
Sparse Core Ops, SparseCore 0:
  11.4 20.9 all-gather.2
  54.2 23.9 reduce-scatter.2
  81.6 18.0 all-gather.4
  153.4 23.9 reduce-scatter.4
where the time goes:
time: 186 us
  waiting for transfers between devices  84.6 us (45%)
  matrix products  66.9 us (36%)
  between operations  14 us (8%)
  other arithmetic  12.4 us (7%)
  local copies, waits for them, and re-layouts  7.65 us (4%)
    dot_general x1, matrix products, local_layer(): jnp.einsum('btf,fd->btd', activation, w_down, preferred_element_type=jnp....  31.2 us
    reduce_scatter x1, waiting for transfers between devices, local_layer(): lax.psum_scatter(attn_part, 'tp', scatter_dimension=1, tiled=True)  23.4 us
    reduce_scatter x1, waiting for transfers between devices, local_layer(): lax.psum_scatter(down_part, 'tp', scatter_dimension=1, tiled=True)  23.3 us
    dot_general x1, matrix products, local_layer(): jnp.einsum('btd,df->btf', normed_mid_all, w_gate, preferred_element_type=...  22.4 us
    all_gather x1, waiting for transfers between devices, local_layer(): normed_all = lax.all_gather(normed, 'tp', axis=1, tiled=True)  19.7 us
    all_gather x1, waiting for transfers between devices, local_layer(): normed_mid_all = lax.all_gather(normed_mid, 'tp', axis=1, tiled=True)  18 us
    dot_general x3, matrix products, project(): jnp.einsum('btd,df->btf', normed, weight, preferred_element_type=jnp.floa...  8.81 us
    unnamed x35, local copies, waits for them, and re-layouts  5.32 us
  transfers between devices with their start and end apart: 4, of which 4 were waited for; matrix products, arithmetic and copies ran while one was open for 1% of the time, Pallas kernels for 0%

commit v1 on v0

v1 whole, which is shorter than its diff:
```python
import jax
import jax.numpy as jnp
from jax import lax
from jax.experimental import pallas as pl
from jax.experimental.pallas import tpu as pltpu
from jax.sharding import PartitionSpec as P

HEAD_DIM = 128
ROPE_THETA = 1000000.0
NORM_EPS = 1e-6
D = 3584
HEADS = 7
QW = HEADS * HEAD_DIM
QKV = QW + 2 * HEAD_DIM
FF = 4736
NC = 7
CW = D // NC
BT = 64
T = 256
TW = 256
GS = 3
DS = 2
F32 = jnp.float32
BF16 = jnp.bfloat16
MESH = pl.DeviceIdType.MESH


def dot(a, b):
    return jnp.dot(a, b, preferred_element_type=F32)


def layer_kernel(x_h, pos_h, g1_h, wq_h, bq_h, wk_h, bk_h, wv_h, bv_h, wo_h, g2_h, wg_h, wu_h, wd_h, freq_h,
                 out_h, kc_h, vc_h,
                 xa, sta, gbuf, ubuf, pbuf, psib, sbuf, xs, obuf, hbuf, cprev, ssum, alpha, xs2, kvb,
                 g1, g2, bq, bk, bv, pos, freq,
                 sm_sem, x_sem, w_sem, wo_sem, g_sem, d_sem, o_sem,
                 xp_s, xp_r, xb_s, xb_r, xf_s, xf_r, st_s, st_r,
                 ps_s, ps_r, sx_s, sx_r, x1_s, x1_r, p2_s, p2_r, s2_s, s2_r):
    tp = lax.axis_index('tp')
    c = lax.div(tp, 2)
    k = lax.rem(tp, 2)
    oc = 1 - c
    ok = 1 - k
    sib = 2 * c + ok
    par = 2 * oc + k

    def remote(src, dst, ssem, rsem, target):
        return pltpu.make_async_remote_copy(src_ref=src, dst_ref=dst, send_sem=ssem, recv_sem=rsem,
                                            device_id={'tp': target}, device_id_type=MESH)

    def x_load(j):
        return pltpu.make_async_copy(x_h.at[0, :, pl.ds(j * CW, CW)], xa.at[j, c, k], x_sem.at[j])

    for j in range(NC):
        x_load(j).start()
    small = [(g1_h, g1), (g2_h, g2), (bq_h, bq), (bk_h, bk), (bv_h, bv), (pos_h, pos), (freq_h, freq)]
    small_cp = [pltpu.make_async_copy(s, d, sm_sem.at[i]) for i, (s, d) in enumerate(small)]
    for cp in small_cp:
        cp.start()

    def g_loads(j, slot):
        rows = pl.ds(pl.multiple_of(j * CW, CW), CW)
        return (pltpu.make_async_copy(wg_h.at[rows], gbuf.at[slot], g_sem.at[slot, 0]),
                pltpu.make_async_copy(wu_h.at[rows], ubuf.at[slot], g_sem.at[slot, 1]))

    def attention_half(wb, wob, qkv):
        def w_loads(j):
            rows = pl.ds(j * CW, CW)
            return (pltpu.make_async_copy(wq_h.at[rows], wb.at[j, :, pl.ds(0, QW)], w_sem.at[j, 0]),
                    pltpu.make_async_copy(wk_h.at[rows], wb.at[j, :, pl.ds(QW, HEAD_DIM)], w_sem.at[j, 1]),
                    pltpu.make_async_copy(wv_h.at[rows], wb.at[j, :, pl.ds(QW + HEAD_DIM, HEAD_DIM)], w_sem.at[j, 2]))

        for j in range(NC):
            for cp in w_loads(j):
                cp.start()
        wo_cp = pltpu.make_async_copy(wo_h, wob, wo_sem)
        wo_cp.start()
        for s in range(GS):
            for cp in g_loads(s, s):
                cp.start()

        barrier = pltpu.get_barrier_semaphore()
        for peer in (sib, par):
            pl.semaphore_signal(barrier, inc=1, device_id={'tp': peer}, device_id_type=MESH)
        pl.semaphore_wait(barrier, 2)

        def x_to_par(j):
            return remote(xa.at[j, c, k], xa.at[j, c, k], xp_s.at[j], xp_r.at[j], par)

        def x_from_par(j):
            return remote(xa.at[j, oc, k], xa.at[j, oc, k], xp_s.at[j], xp_r.at[j], par)

        def x_to_sib(j):
            return remote(xa.at[j, c, k], xa.at[j, c, k], xb_s.at[j], xb_r.at[j], sib)

        def x_from_sib(j):
            return remote(xa.at[j, c, ok], xa.at[j, c, ok], xb_s.at[j], xb_r.at[j], sib)

        def x_forward(j):
            return remote(xa.at[j, oc, k], xa.at[j, oc, k], xf_s.at[j], xf_r.at[j], sib)

        def x_forwarded(j):
            return remote(xa.at[j, oc, ok], xa.at[j, oc, ok], xf_s.at[j], xf_r.at[j], sib)

        x_load(0).wait()
        x_to_par(0).start()
        x_to_sib(0).start()
        square = jnp.zeros((BT, CW), F32)
        for j in range(NC):
            if j:
                x_load(j).wait()
            part = xa[j, c, k].astype(F32)
            square = square + part * part
        mean = jnp.sum(square, axis=-1, keepdims=True) / D
        inv = jnp.broadcast_to(lax.rsqrt(mean + NORM_EPS), (BT, 128))
        sta[c, k] = jnp.transpose(jnp.concatenate([inv, inv], axis=0))[:8]
        st_par = remote(sta.at[c, k], sta.at[c, k], st_s.at[0], st_r.at[0], par)
        st_par.start()
        st_sib = remote(sta.at[c, k], sta.at[c, k], st_s.at[1], st_r.at[1], sib)
        st_sib.start()
        for j in range(1, NC):
            x_to_par(j).start()
            x_to_sib(j).start()

        for cp in small_cp:
            cp.wait()
        pos_col = jnp.transpose(jnp.broadcast_to(pos[...].astype(F32), (HEAD_DIM, T)))
        angles = pos_col * freq[...]
        cosine = jnp.cos(angles)
        sine = jnp.sin(angles)
        lane = lax.broadcasted_iota(jnp.int32, (T, HEAD_DIM), 1)
        sine = jnp.where(lane < HEAD_DIM // 2, -sine, sine)

        remote(sta.at[oc, k], sta.at[oc, k], st_s.at[0], st_r.at[0], par).wait_recv()
        st_fwd = remote(sta.at[oc, k], sta.at[oc, k], st_s.at[2], st_r.at[2], sib)
        st_fwd.start()
        remote(sta.at[c, ok], sta.at[c, ok], st_s.at[1], st_r.at[1], sib).wait_recv()
        remote(sta.at[oc, ok], sta.at[oc, ok], st_s.at[2], st_r.at[2], sib).wait_recv()
        for cc in range(2):
            for kk in range(2):
                row = jnp.broadcast_to(sta[cc, kk][0:1], (128, 128))
                cprev[pl.ds((cc * 2 + kk) * BT, BT), :] = jnp.transpose(row)[:BT]
        qkv[...] = jnp.zeros_like(qkv)

        def project(j):
            x_from_sib(j).wait_recv()
            x_forwarded(j).wait_recv()
            for cp in w_loads(j):
                cp.wait()
            values = xa[j].reshape(T, CW).astype(F32)
            scale = jnp.concatenate([cprev[...]] * (CW // 128), axis=1)
            gain = g1[:, pl.ds(pl.multiple_of(j * CW, CW), CW)].astype(F32)
            hbuf[...] = (values * scale * gain).astype(BF16)
            qkv[...] += dot(hbuf[...], wb[j])

        x_from_par(0).wait_recv()
        x_forward(0).start()

        @pl.loop(1, NC)
        def _(j):
            x_from_par(j).wait_recv()
            x_forward(j).start()
            project(j - 1)

        project(NC - 1)

        def rotate(u):
            return u * cosine + pltpu.roll(u, HEAD_DIM // 2, 1) * sine

        key = rotate(qkv[:, pl.ds(QW, HEAD_DIM)] + bk[...].astype(F32)).astype(BF16)
        value = (qkv[:, pl.ds(QW + HEAD_DIM, HEAD_DIM)] + bv[...].astype(F32)).astype(BF16)
        kvb[0] = key
        kvb[1] = value
        k_out = pltpu.make_async_copy(kvb.at[0], kc_h, o_sem.at[NC])
        v_out = pltpu.make_async_copy(kvb.at[1], vc_h, o_sem.at[NC + 1])
        k_out.start()
        v_out.start()
        half = T // 2
        row_i = lax.broadcasted_iota(jnp.int32, (half, half), 0)
        col_i = lax.broadcasted_iota(jnp.int32, (half, half), 1)
        causal = row_i >= col_i
        for h in range(HEADS):
            cols = pl.ds(h * HEAD_DIM, HEAD_DIM)
            query = rotate(qkv[:, cols] + bq[:, cols].astype(F32)).astype(BF16)
            for r in range(2):
                width = half * (r + 1)
                scores = lax.dot_general(query[r * half:(r + 1) * half], key[:width], (((1,), (1,)), ((), ())),
                                         preferred_element_type=F32) * (HEAD_DIM ** -0.5)
                last = jnp.where(causal, scores[:, width - half:], -1e30)
                scores = last if r == 0 else jnp.concatenate([scores[:, :half], last], axis=1)
                weights = jnp.exp(scores - jnp.max(scores, axis=-1, keepdims=True))
                probs = (weights / jnp.sum(weights, axis=-1, keepdims=True)).astype(BF16)
                obuf[pl.ds(r * half, half), cols] = dot(probs, value[:width]).astype(BF16)

        wo_cp.wait()

        @pl.loop(0, NC)
        def _(j):
            cols = pl.ds(pl.multiple_of(j * CW, CW), CW)
            pbuf[j] = dot(obuf[...], wob[:, cols]).astype(BF16).reshape(2, 2, BT, CW)
            p_send(j).start()

        @pl.loop(0, NC)
        def _(j):
            x_to_par(j).wait_send()
            x_to_sib(j).wait_send()
            x_forward(j).wait_send()

        st_par.wait_send()
        st_sib.wait_send()
        st_fwd.wait_send()
        k_out.wait()
        v_out.wait()

    def p_send(j):
        return remote(pbuf.at[j, :, ok], psib.at[j], ps_s.at[j], ps_r.at[j], sib)

    pl.run_scoped(attention_half,
                  pltpu.VMEM((NC, CW, QKV), BF16), pltpu.VMEM((QW, D), BF16), pltpu.VMEM((T, QKV), F32))

    def mlp_half(accg, accu, act, dbuf):
        def d_load(j, slot):
            cols = pl.ds(pl.multiple_of(j * CW, CW), CW)
            return pltpu.make_async_copy(wd_h.at[:, cols], dbuf.at[slot], d_sem.at[slot])

        for s in range(DS):
            d_load(s, s).start()

        def s_send(j):
            return remote(sbuf.at[j], xs.at[j], sx_s.at[j], sx_r.at[j], par)

        def x1_send(j):
            return remote(xa.at[j, :, k], xa.at[j, :, k], x1_s.at[j], x1_r.at[j], sib)

        def x1_recv(j):
            return remote(xa.at[j, :, ok], xa.at[j, :, ok], x1_s.at[j], x1_r.at[j], sib)

        @pl.loop(0, NC)
        def _(j):
            p_send(j).wait_recv()
            sbuf[j] = (pbuf[j, :, k].astype(F32) + psib[j].astype(F32)).astype(BF16)
            s_send(j).start()

        def residual(j):
            s_send(j).wait_recv()
            total = sbuf[j].astype(F32) + xs[j].astype(F32)
            xa[j, :, k] = (xa[j, :, k].astype(F32) + total).astype(BF16)
            x1_send(j).start()

        def normalise(j, first):
            x1_recv(j).wait_recv()
            values = xa[j].reshape(T, CW).astype(F32)
            row_sum = jnp.sum(values * values, axis=-1, keepdims=True)
            if not first:
                row_sum = row_sum + ssum[...]
            ssum[...] = row_sum
            scale = lax.rsqrt(row_sum / ((j + 1) * CW) + NORM_EPS)
            wide = jnp.broadcast_to(scale, (T, 128))
            if not first:
                alpha[...] = wide / cprev[...]
            cprev[...] = wide
            gain = g2[:, pl.ds(pl.multiple_of(j * CW, CW), CW)].astype(F32)
            hbuf[...] = (values * scale * gain).astype(BF16)

        def put(mode, cols, dg, du):
            w = dg.shape[1]
            if mode != 'first':
                al = jnp.concatenate([alpha[...]] * (w // 128), axis=1)
                dg = accg[:, cols] * al + dg
                du = accu[:, cols] * al + du
            if mode == 'last':
                act[:, cols] = (dg / (1.0 + jnp.exp(-dg)) * du).astype(BF16)
            else:
                accg[:, cols] = dg
                accu[:, cols] = du

        def tiles(slot, mode, lo, hi):
            for n in range(lo, hi):
                cols = pl.ds(n * TW, TW)
                put(mode, cols, dot(hbuf[...], gbuf[slot, :, cols]), dot(hbuf[...], ubuf[slot, :, cols]))

        def tail(slot, mode):
            cols = pl.ds(FF - 128, 128)
            both = jnp.concatenate([gbuf[slot, :, cols], ubuf[slot, :, cols]], axis=1)
            res = dot(hbuf[...], both)
            put(mode, cols, res[:, :128], res[:, 128:])

        NT = FF // TW
        CUT = 11

        def gate_up(j, slot, mode):
            normalise(j, mode == 'first')
            for cp in g_loads(j, slot):
                cp.wait()
            tiles(slot, mode, 0, CUT)
            if mode != 'last':
                residual(j + 1)
            tiles(slot, mode, CUT, NT)
            tail(slot, mode)

        residual(0)
        gate_up(0, 0, 'first')
        for cp in g_loads(GS, 0):
            cp.start()

        @pl.loop(1, NC - 1)
        def _(j):
            slot = lax.rem(j, GS)
            gate_up(j, slot, 'mid')

            @pl.when(j + GS < NC)
            def _():
                for cp in g_loads(j + GS, slot):
                    cp.start()

        gate_up(NC - 1, (NC - 1) % GS, 'last')

        @pl.loop(0, NC)
        def _(j):
            p_send(j).wait_send()
            s_send(j).wait_send()

        def p2_send(j):
            return remote(pbuf.at[j, :, ok], psib.at[j], p2_s.at[j], p2_r.at[j], sib)

        def s2_send(j):
            return remote(sbuf.at[j, oc], xs2.at[j], s2_s.at[j], s2_r.at[j], par)

        def out_copy(j):
            cols = pl.ds(pl.multiple_of(j * CW, CW), CW)
            return pltpu.make_async_copy(sbuf.at[j, c], out_h.at[0, :, cols], o_sem.at[j])

        def down(j):
            slot = lax.rem(j, DS)
            d_load(j, slot).wait()
            pbuf[j] = dot(act[...], dbuf[slot]).astype(BF16).reshape(2, 2, BT, CW)
            p2_send(j).start()

        def chip_sum(j):
            p2_send(j).wait_recv()
            sbuf[j, oc] = (pbuf[j, oc, k].astype(F32) + psib[j, oc].astype(F32)).astype(BF16)
            s2_send(j).start()

        def finish(j):
            s2_send(j).wait_recv()
            total = pbuf[j, c, k].astype(F32) + psib[j, c].astype(F32) + xs2[j].astype(F32)
            sbuf[j, c] = (xa[j, c, k].astype(F32) + total).astype(BF16)
            out_copy(j).start()

        down(0)
        d_load(DS, 0).start()

        @pl.loop(1, NC)
        def _(j):
            down(j)

            @pl.when(j + DS < NC)
            def _():
                d_load(j + DS, lax.rem(j, DS)).start()

            chip_sum(j - 1)

        chip_sum(NC - 1)

        @pl.loop(0, NC)
        def _(j):
            finish(j)

        @pl.loop(0, NC)
        def _(j):
            x1_send(j).wait_send()
            p2_send(j).wait_send()
            s2_send(j).wait_send()
            out_copy(j).wait()

    pl.run_scoped(mlp_half,
                  pltpu.VMEM((T, FF), F32), pltpu.VMEM((T, FF), F32), pltpu.VMEM((T, FF), BF16),
                  pltpu.VMEM((DS, FF, CW), BF16))


def solution(mesh):
    def local_layer(hidden, positions, gain_attn, w_q, b_q, w_k, b_k, w_v, b_v, w_o, gain_mlp, w_gate, w_up, w_down):
        half = HEAD_DIM // 2
        freq = ROPE_THETA ** (-jnp.arange(half, dtype=F32) / half)
        freq = jnp.concatenate([freq, freq]).reshape(1, HEAD_DIM)
        dma = pltpu.SemaphoreType.DMA
        sems = [dma((7,)), dma((NC,)), dma((NC, 3)), dma, dma((GS, 2)), dma((DS,)), dma((NC + 2,)),
                dma((NC,)), dma((NC,)), dma((NC,)), dma((NC,)), dma((NC,)), dma((NC,)), dma((3,)), dma((3,))]
        sems += [dma((NC,)) for _ in range(10)]
        vm = pltpu.VMEM
        out, kc, vc = pl.pallas_call(
            layer_kernel,
            out_shape=(jax.ShapeDtypeStruct((1, BT, D), BF16), jax.ShapeDtypeStruct((T, HEAD_DIM), BF16),
                       jax.ShapeDtypeStruct((T, HEAD_DIM), BF16)),
            in_specs=[pl.BlockSpec(memory_space=pl.ANY)] * 15,
            out_specs=(pl.BlockSpec(memory_space=pl.ANY),) * 3,
            scratch_shapes=[
                vm((NC, 2, 2, BT, CW), BF16), vm((2, 2, 8, 128), F32),
                vm((GS, CW, FF), BF16), vm((GS, CW, FF), BF16),
                vm((NC, 2, 2, BT, CW), BF16), vm((NC, 2, BT, CW), BF16), vm((NC, 2, BT, CW), BF16), vm((NC, 2, BT, CW), BF16),
                vm((T, QW), BF16), vm((T, CW), BF16), vm((T, 128), F32), vm((T, 1), F32),
                vm((T, 128), F32), vm((NC, BT, CW), BF16), vm((2, T, HEAD_DIM), BF16),
                vm((1, D), BF16), vm((1, D), BF16), vm((1, QW), BF16), vm((1, HEAD_DIM), BF16), vm((1, HEAD_DIM), BF16),
                vm((1, T), jnp.int32), vm((1, HEAD_DIM), F32),
            ] + sems,
            compiler_params=pltpu.CompilerParams(collective_id=0, has_side_effects=True, vmem_limit_bytes=67043328),
            name='layer',
        )(hidden, positions, gain_attn.reshape(1, D), w_q, b_q.reshape(1, QW), w_k, b_k.reshape(1, HEAD_DIM), w_v,
          b_v.reshape(1, HEAD_DIM), w_o, gain_mlp.reshape(1, D), w_gate, w_up, w_down, freq)
        return out, kc.reshape(1, T, 1, HEAD_DIM), vc.reshape(1, T, 1, HEAD_DIM)

    token_rows = P('dp', 'tp', None)
    col_split = P(None, 'tp')
    row_split = P('tp', None)
    vec_split = P('tp')
    replicated = P(None)
    cache_spec = P('dp', None, 'tp', None)
    in_specs = (token_rows, P('dp', None), replicated, col_split, vec_split, col_split, vec_split, col_split, vec_split, row_split, replicated, col_split, col_split, row_split)
    out_specs = (token_rows, cache_spec, cache_spec)
    return jax.shard_map(local_layer, mesh=mesh, in_specs=in_specs, out_specs=out_specs, check_vma=False)
```

time: 186 us -> 82.1 us (0.44)
  waiting for transfers between devices: 84.6 us -> 0 us
  Pallas kernels: 0 us -> 71.7 us
  matrix products: 66.9 us -> 0 us
  between operations: 14 us -> 0.64 us
  other arithmetic: 12.4 us -> 0.66 us
    pallas_call x0 -> x1, Pallas kernels: none -> 71.7 us  [local_layer(): pl.pallas_call(layer_kernel, out_shape=(jax.ShapeDtypeStruct((1, BT, D),...]
    dot_general x8 -> x0, matrix products: 66.9 us -> none  [the longest x1 31.2 us: local_layer(): jnp.einsum('btf,fd->btd', activation, w_down, preferred_element_type=jnp....]
    reduce_scatter x2 -> x0, waiting for transfers between devices: 46.8 us -> none  [the longest x1 23.4 us: local_layer(): lax.psum_scatter(attn_part, 'tp', scatter_dimension=1, tiled=True)]
    all_gather x2 -> x0, waiting for transfers between devices: 37.7 us -> none  [the longest x1 19.7 us: local_layer(): normed_all = lax.all_gather(normed, 'tp', axis=1, tiled=True)]
    convert_element_type x9 -> x0, other arithmetic: 6.6 us -> none  [the longest x2 3.92 us: rms_norm(): (values_f32 * inv_rms * gain.astype(jnp.float32)).astype(jnp.bfloat16)]
    reshape x0 -> x3, local copies, waits for them, and re-layouts: none -> 3.87 us  [the longest x1 1.3 us: local_layer(): gain_attn.reshape(1, D)]
    reduce_sum x3 -> x0, other arithmetic: 2.8 us -> none  [the longest x2 2.54 us: rms_norm(): jnp.mean(values_f32 * values_f32, axis=-1, keepdims=True) + NORM_EPS]
    unnamed x35 -> x3, local copies, waits for them, and re-layouts: 5.32 us -> 4.76 us
  transfers between devices with their start and end apart: 4 -> 0, of which waited for: 4 -> 0; matrix products, arithmetic and copies ran while one was open for 1% -> 0% of each run, Pallas kernels for 0% -> 0%
where the time goes in v1:
time: 82.1 us; the launch traced here: 81.6 us
  Pallas kernels  71.7 us (87%)
  local copies, waits for them, and re-layouts  8.63 us (11%)
    pallas_call x1, Pallas kernels, local_layer(): pl.pallas_call(layer_kernel, out_shape=(jax.ShapeDtypeStruct((1, BT, D),...  71.7 us
    unnamed x3, local copies, waits for them, and re-layouts  4.76 us

profile of v1, /device:TPU:0, one launch (start us, length us, event | category | flops | bytes accessed | tf_op | source)
XLA Modules:
  0.0 81.6 jit_solution(10875222615058468236)
XLA Ops:
  0.6 0.7 maximum_bitcast_fusion.freq_h
  1.3 1.3 %reshape.31.bq_h = bf16[1,896]{1,0:T(2,128)(2,1)} reshape(bf16[896]{0:T(1024)(128)(2,1)} %param.18) | data formatting | bytes 3584 | tf_op jit(solution)/shard_map/reshape | solution.py:408
  2.6 1.3 %reshape.30.g1_h = bf16[1,3584]{1,0:T(2,128)(2,1)} reshape(bf16[3584]{0:T(1024)(128)(2,1)} %param.16) | data formatting | bytes 14336 | tf_op jit(solution)/shard_map/reshape | solution.py:408
  3.9 1.3 %reshape.34.g2_h = bf16[1,3584]{1,0:T(2,128)(2,1)} reshape(bf16[3584]{0:T(1024)(128)(2,1)} %param.24) | data formatting | bytes 14336 | tf_op jit(solution)/shard_map/reshape | solution.py:409
  5.2 71.7 %layer.1 = (bf16[1,64,3584]{2,1,0:T(8,128)(2,1)}, bf16[256,128]{1,0:T(8,128)(2,1)}, bf16[256,128]{1,0:T(8,128)(2,1)}) custom-call(bf16[1,64,3584]{2,1,0:T(8,128)(2,1)} %x_h.1, s32[1,256]{1,0:T(1,128)} %pos_h.1, bf16[1,3584]{1,0:T(2,128)(2,1)} %reshape.30.g1_h, bf16[3584,896]{1,0:T(8,128)(2,1)} %wq_h.1, bf16[1,896]{1,0:T(2,128)(2,1)} %reshape.31.bq_h, ...), custom_call_target="tpu_custom_call" | custom-call | tf_op jit(solution)/shard_map/layer/pallas_call | solution.py:391
  76.8 1.8 %copy.20 = bf16[1,64,3584]{2,1,0:T(8,128)(2,1)} copy(bf16[1,64,3584]{2,1,0:T(8,128)(2,1)} %get-tuple-element.12) | data formatting | bytes 917504
  78.6 1.5 %copy.21 = bf16[1,256,1,128]{3,1,2,0:T(8,128)(2,1)} copy(bf16[1,256,1,128]{3,1,2,0:T(8,128)(2,1)} %bitcast.7) | data formatting | bytes 131072
  80.1 1.5 %copy.22 = bf16[1,256,1,128]{3,1,2,0:T(8,128)(2,1)} copy(bf16[1,256,1,128]{3,1,2,0:T(8,128)(2,1)} %bitcast.6) | data formatting | bytes 131072
  (1 shorter events, 0.0 us)

commit v2 on v1

v2 whole, which is shorter than its diff:
```python
import jax
import jax.numpy as jnp
import numpy as np
from jax import lax
from jax.experimental import pallas as pl
from jax.experimental.pallas import tpu as pltpu
from jax.sharding import PartitionSpec as P

HEAD_DIM = 128
ROPE_THETA = 1000000.0
NORM_EPS = 1e-6
D = 3584
HEADS = 7
QW = HEADS * HEAD_DIM
QKV = QW + 2 * HEAD_DIM
FF = 4736
NC = 7
CW = D // NC
BT = 64
T = 256
TW = 256
GH = 5
DS = 3
HW = CW // 2
UNITS = tuple((j, 0, CW) for j in range(NC))
NU = len(UNITS)
OUTS = tuple((j, 0, CW) for j in range(NC - 1)) + ((NC - 1, 0, HW), (NC - 1, HW, HW))
NO = len(OUTS)
F32 = jnp.float32
BF16 = jnp.bfloat16
MESH = pl.DeviceIdType.MESH


def add(parts):
    first, second = parts
    return first + second


def dot(a, b):
    return jnp.dot(a, b, preferred_element_type=F32)


def row(ref, start, size):
    if not isinstance(start, int):
        start = pl.multiple_of(start, size)
    return ref[pl.ds(start, size)].astype(F32).reshape(1, size)


def result_kernel(out_i, kc_i, vc_i, out_o, kc_o, vc_o, outb, kvb, i_sem, o_sem):
    loads = [(out_i.at[0, :, pl.ds(j * CW, CW)], outb.at[j]) for j in range(NC)] + [(kc_i, kvb.at[0]), (vc_i, kvb.at[1])]
    stores = [(outb.at[j], out_o.at[0, :, pl.ds(j * CW, CW)]) for j in range(NC)] + [(kvb.at[0], kc_o), (kvb.at[1], vc_o)]
    loads = [pltpu.make_async_copy(s, d, i_sem.at[i]) for i, (s, d) in enumerate(loads)]
    stores = [pltpu.make_async_copy(s, d, o_sem.at[i]) for i, (s, d) in enumerate(stores)]
    for cp in loads:
        cp.start()
    for load, store in zip(loads, stores):
        load.wait()
        store.start()
    for store in stores:
        store.wait()


def layer_kernel(x_h, pos_h, g1_h, wq_h, bq_h, wk_h, bk_h, wv_h, bv_h, wo_h, g2_h, wg_h, wu_h, wd_h, freq_h,
                 out_h, kc_h, vc_h,
                 xa, sta, gbuf, ubuf, pbuf, psib, sbuf, xs, obuf, hbuf, cprev, ssum, alpha, xs2,
                 g1, g2, bq, bk, bv, pos, freq,
                 sm_sem, x_sem, w_sem, wo_sem, g_sem, d_sem, o_sem,
                 xp_s, xp_r, xb_s, xb_r, xf_s, xf_r, st_s, st_r,
                 ps_s, ps_r, sx_s, sx_r, x1_s, x1_r, p2_s, p2_r, s2_s, s2_r):
    tp = lax.axis_index('tp')
    c = lax.div(tp, 2)
    k = lax.rem(tp, 2)
    oc = 1 - c
    ok = 1 - k
    sib = 2 * c + ok
    par = 2 * oc + k

    def remote(src, dst, ssem, rsem, target):
        return pltpu.make_async_remote_copy(src_ref=src, dst_ref=dst, send_sem=ssem, recv_sem=rsem,
                                            device_id={'tp': target}, device_id_type=MESH)

    def x_load(j):
        return pltpu.make_async_copy(x_h.at[0, :, pl.ds(j * CW, CW)], xa.at[j, c, k], x_sem.at[j])

    for j in range(NC):
        x_load(j).start()
    small = [(g1_h, g1), (g2_h, g2), (bq_h, bq), (bk_h, bk), (bv_h, bv), (pos_h, pos), (freq_h, freq)]
    small_cp = [pltpu.make_async_copy(s, d, sm_sem.at[i]) for i, (s, d) in enumerate(small)]
    for cp in small_cp:
        cp.start()

    def g_loads(i):
        slot = lax.rem(i, GH)
        rows = pl.ds(pl.multiple_of(i * HW, HW), HW)
        return (pltpu.make_async_copy(wg_h.at[rows], gbuf.at[slot], g_sem.at[slot, 0]),
                pltpu.make_async_copy(wu_h.at[rows], ubuf.at[slot], g_sem.at[slot, 1]))

    def attention_half(wb, wob, qkv):
        def w_loads(j):
            rows = pl.ds(j * CW, CW)
            return (pltpu.make_async_copy(wq_h.at[rows], wb.at[j, :, pl.ds(0, QW)], w_sem.at[j, 0]),
                    pltpu.make_async_copy(wk_h.at[rows], wb.at[j, :, pl.ds(QW, HEAD_DIM)], w_sem.at[j, 1]),
                    pltpu.make_async_copy(wv_h.at[rows], wb.at[j, :, pl.ds(QW + HEAD_DIM, HEAD_DIM)], w_sem.at[j, 2]))

        for j in range(NC):
            for cp in w_loads(j):
                cp.start()
        wo_cp = pltpu.make_async_copy(wo_h, wob, wo_sem)
        wo_cp.start()
        for i in range(GH):
            for cp in g_loads(i):
                cp.start()

        barrier = pltpu.get_barrier_semaphore()
        for peer in (sib, par):
            pl.semaphore_signal(barrier, inc=1, device_id={'tp': peer}, device_id_type=MESH)
        pl.semaphore_wait(barrier, 2)

        def x_to_par(j):
            return remote(xa.at[j, c, k], xa.at[j, c, k], xp_s.at[j], xp_r.at[j], par)

        def x_from_par(j):
            return remote(xa.at[j, oc, k], xa.at[j, oc, k], xp_s.at[j], xp_r.at[j], par)

        def x_to_sib(j):
            return remote(xa.at[j, c, k], xa.at[j, c, k], xb_s.at[j], xb_r.at[j], sib)

        def x_from_sib(j):
            return remote(xa.at[j, c, ok], xa.at[j, c, ok], xb_s.at[j], xb_r.at[j], sib)

        def x_forward(j):
            return remote(xa.at[j, oc, k], xa.at[j, oc, k], xf_s.at[j], xf_r.at[j], sib)

        def x_forwarded(j):
            return remote(xa.at[j, oc, ok], xa.at[j, oc, ok], xf_s.at[j], xf_r.at[j], sib)

        x_load(0).wait()
        x_to_par(0).start()
        x_to_sib(0).start()
        square = jnp.zeros((BT, CW), F32)
        for j in range(NC):
            if j:
                x_load(j).wait()
            part = xa[j, c, k].astype(F32)
            square = square + part * part
        mean = jnp.sum(square, axis=-1, keepdims=True) / D
        inv = jnp.broadcast_to(lax.rsqrt(mean + NORM_EPS), (BT, 128))
        sta[c, k] = jnp.transpose(jnp.concatenate([inv, inv], axis=0))[:8]
        st_par = remote(sta.at[c, k], sta.at[c, k], st_s.at[0], st_r.at[0], par)
        st_par.start()
        st_sib = remote(sta.at[c, k], sta.at[c, k], st_s.at[1], st_r.at[1], sib)
        st_sib.start()
        for j in range(1, NC):
            x_to_par(j).start()
            x_to_sib(j).start()

        for cp in small_cp:
            cp.wait()
        pos_col = jnp.transpose(jnp.broadcast_to(pos[...].astype(F32), (HEAD_DIM, T)))
        angles = pos_col * freq[...]
        cosine = jnp.cos(angles)
        sine = jnp.sin(angles)
        lane = lax.broadcasted_iota(jnp.int32, (T, HEAD_DIM), 1)
        sine = jnp.where(lane < HEAD_DIM // 2, -sine, sine)

        remote(sta.at[oc, k], sta.at[oc, k], st_s.at[0], st_r.at[0], par).wait_recv()
        st_fwd = remote(sta.at[oc, k], sta.at[oc, k], st_s.at[2], st_r.at[2], sib)
        st_fwd.start()
        remote(sta.at[c, ok], sta.at[c, ok], st_s.at[1], st_r.at[1], sib).wait_recv()
        remote(sta.at[oc, ok], sta.at[oc, ok], st_s.at[2], st_r.at[2], sib).wait_recv()
        for cc in range(2):
            for kk in range(2):
                wide = jnp.broadcast_to(sta[cc, kk][0:1], (128, 128))
                cprev[pl.ds((cc * 2 + kk) * BT, BT), :] = jnp.transpose(wide)[:BT]
        qkv[...] = jnp.zeros_like(qkv)

        def project(j):
            x_from_sib(j).wait_recv()
            x_forwarded(j).wait_recv()
            for cp in w_loads(j):
                cp.wait()
            values = xa[j].reshape(T, CW).astype(F32)
            scale = jnp.concatenate([cprev[...]] * (CW // 128), axis=1)
            gain = row(g1, j * CW, CW)
            hbuf[...] = (values * scale * gain).astype(BF16)
            qkv[...] += dot(hbuf[...], wb[j])

        x_from_par(0).wait_recv()
        x_forward(0).start()

        @pl.loop(1, NC)
        def _(j):
            x_from_par(j).wait_recv()
            x_forward(j).start()
            project(j - 1)

        project(NC - 1)

        def rotate(u):
            return u * cosine + pltpu.roll(u, HEAD_DIM // 2, 1) * sine

        key = rotate(qkv[:, pl.ds(QW, HEAD_DIM)] + row(bk, 0, HEAD_DIM)).astype(BF16)
        value = (qkv[:, pl.ds(QW + HEAD_DIM, HEAD_DIM)] + row(bv, 0, HEAD_DIM)).astype(BF16)
        key_lanes, value_lanes = pl.ds(0, HEAD_DIM), pl.ds(HEAD_DIM, HEAD_DIM)
        hbuf[:, key_lanes] = key
        hbuf[:, value_lanes] = value
        k_out = pltpu.make_async_copy(hbuf.at[:, key_lanes], kc_h, o_sem.at[NO])
        v_out = pltpu.make_async_copy(hbuf.at[:, value_lanes], vc_h, o_sem.at[NO + 1])
        k_out.start()
        v_out.start()
        half = T // 2
        rows = HEADS * half
        row_i = lax.rem(lax.broadcasted_iota(jnp.int32, (rows, half), 0), half)
        causal = row_i >= lax.broadcasted_iota(jnp.int32, (rows, half), 1)
        query = [rotate(qkv[:, pl.ds(h * HEAD_DIM, HEAD_DIM)] + row(bq, h * HEAD_DIM, HEAD_DIM)).astype(BF16)
                 for h in range(HEADS)]
        for r in range(2):
            width = half * (r + 1)
            stacked = jnp.concatenate([q[r * half:(r + 1) * half] for q in query], axis=0)
            scores = lax.dot_general(stacked, key[:width], (((1,), (1,)), ((), ())),
                                     preferred_element_type=F32) * (HEAD_DIM ** -0.5)
            last = jnp.where(causal, scores[:, width - half:], -1e30)
            scores = last if r == 0 else jnp.concatenate([scores[:, :half], last], axis=1)
            weights = jnp.exp(scores - jnp.max(scores, axis=-1, keepdims=True))
            probs = (weights * (1.0 / jnp.sum(weights, axis=-1, keepdims=True))).astype(BF16)
            out = dot(probs, value[:width]).astype(BF16)
            for h in range(HEADS):
                obuf[pl.ds(r * half, half), pl.ds(h * HEAD_DIM, HEAD_DIM)] = out[h * half:(h + 1) * half]

        wo_cp.wait()

        lag = 3
        for u, (j, lo, w) in enumerate(UNITS):
            part = dot(obuf[...], wob[:, pl.ds(j * CW + lo, w)]).astype(BF16)
            pbuf[j, :, :, :, pl.ds(lo, w)] = part.reshape(2, 2, BT, w)
            p_send(u, j, lo, w).start()
            if u >= lag:
                chip_partial(u - lag)
        for u in range(NU - lag, NU):
            chip_partial(u)

        @pl.loop(0, NC)
        def _(j):
            x_to_par(j).wait_send()
            x_to_sib(j).wait_send()
            x_forward(j).wait_send()

        st_par.wait_send()
        st_sib.wait_send()
        st_fwd.wait_send()
        k_out.wait()
        v_out.wait()

    def p_send(u, j, lo, w):
        lanes = pl.ds(lo, w)
        return remote(pbuf.at[j, :, ok, :, lanes], psib.at[j, :, :, lanes], ps_s.at[u], ps_r.at[u], sib)

    def s_send(u, j, lo, w):
        lanes = pl.ds(lo, w)
        return remote(sbuf.at[j, :, :, lanes], xs.at[j, :, :, lanes], sx_s.at[u], sx_r.at[u], par)

    def chip_partial(u):
        j, lo, w = UNITS[u]
        lanes = pl.ds(lo, w)
        p_send(u, j, lo, w).wait_recv()
        sbuf[j, :, :, lanes] = (pbuf[j, :, k, :, lanes].astype(F32) + psib[j, :, :, lanes].astype(F32)).astype(BF16)
        s_send(u, j, lo, w).start()

    pl.run_scoped(attention_half,
                  pltpu.VMEM((NC, CW, QKV), BF16), pltpu.VMEM((QW, D), BF16), pltpu.VMEM((T, QKV), F32))

    def mlp_half(accg, accu, act, dbuf):
        def d_load(j, slot):
            cols = pl.ds(pl.multiple_of(j * CW, CW), CW)
            return pltpu.make_async_copy(wd_h.at[:, cols], dbuf.at[slot], d_sem.at[slot])

        for s in range(DS):
            d_load(s, s).start()

        def x1_send(u, j, lo, w):
            part = xa.at[j, :, k, :, pl.ds(lo, w)]
            return remote(part, part, x1_s.at[u], x1_r.at[u], sib)

        def x1_recv(u, j, lo, w):
            part = xa.at[j, :, ok, :, pl.ds(lo, w)]
            return remote(part, part, x1_s.at[u], x1_r.at[u], sib)

        def residual(u, j, lo, w):
            lanes = pl.ds(lo, w)
            s_send(u, j, lo, w).wait_recv()
            total = sbuf[j, :, :, lanes].astype(F32) + xs[j, :, :, lanes].astype(F32)
            xa[j, :, k, :, lanes] = (xa[j, :, k, :, lanes].astype(F32) + total).astype(BF16)
            x1_send(u, j, lo, w).start()

        def normalise(u):
            values = xa[u].reshape(T, CW).astype(F32)
            row_sum = jnp.sum(values * values, axis=-1, keepdims=True)
            first = isinstance(u, int) and u == 0
            if not first:
                row_sum = row_sum + ssum[...]
            ssum[...] = row_sum
            scale = lax.rsqrt(row_sum / ((u + 1) * CW) + NORM_EPS)
            wide = jnp.broadcast_to(scale, (T, 128))
            if not first:
                alpha[...] = wide / cprev[...]
            cprev[...] = wide
            hbuf[...] = (values * scale * row(g2, u * CW, CW)).astype(BF16)

        def put(mode, rows, cols, dg, du):
            w = dg.shape[1]
            if mode != 'first':
                al = jnp.concatenate([alpha[rows, :]] * (w // 128), axis=1)
                dg = accg[rows, cols] * al + dg
                du = accu[rows, cols] * al + du
            if mode == 'last':
                act[rows, cols] = (dg / (1.0 + jnp.exp(-dg)) * du).astype(BF16)
            else:
                accg[rows, cols] = dg
                accu[rows, cols] = du

        def tiles(halves, mode, lo, hi):
            for n in range(lo, hi):
                cols = pl.ds(n * TW, TW)
                dg, du = [add([dot(hbuf[:, pl.ds(i * HW, HW)], ref[slot, :, cols]) for i, slot in enumerate(halves)])
                          for ref in (gbuf, ubuf)]
                put(mode, pl.ds(0, T), cols, dg, du)

        def tail(halves, mode):
            cols = pl.ds(FF - 128, 128)
            weight = [jnp.concatenate([gbuf[slot, :, cols], ubuf[slot, :, cols]], axis=1) for slot in halves]
            for r in range(2):
                rows = pl.ds(r * 2 * BT, 2 * BT)
                res = add([dot(hbuf[rows, pl.ds(i * HW, HW)], w) for i, w in enumerate(weight)])
                put(mode, rows, cols, res[:, :128], res[:, 128:])

        NT = FF // TW

        def gate_up(u, mode, cut):
            x1_recv(u, u, 0, CW).wait_recv()
            for i in range(2):
                for cp in g_loads(2 * u + i):
                    cp.wait()
            halves = [lax.rem(2 * u + i, GH) for i in range(2)]
            normalise(u)
            if mode == 'last':
                tiles(halves, mode, 0, NT)
            else:
                tiles(halves, mode, 0, cut)
                residual(u + 1, u + 1, 0, CW)
                tiles(halves, mode, cut, NT)
            tail(halves, mode)

        def refill(i):
            for cp in g_loads(i):
                cp.start()

        unit = [(u,) + UNITS[u] for u in range(NU)]
        residual(*unit[0])
        gate_up(0, 'first', 13)
        for i in range(2):
            refill(GH + i)

        @pl.loop(1, NC - 1)
        def _(u):
            gate_up(u, 'mid', 9)
            for i in range(2):
                @pl.when(2 * u + i + GH < 2 * NC)
                def _():
                    refill(2 * u + i + GH)

        gate_up(NC - 1, 'last', NT)

        for u in range(NU):
            p_send(*unit[u]).wait_send()
            s_send(*unit[u]).wait_send()

        def p2_send(u, j, lo, w):
            lanes = pl.ds(lo, w)
            return remote(pbuf.at[j, :, ok, :, lanes], psib.at[j, :, :, lanes], p2_s.at[u], p2_r.at[u], sib)

        def s2_send(u, j, lo, w):
            lanes = pl.ds(lo, w)
            return remote(sbuf.at[j, oc, :, lanes], xs2.at[j, :, lanes], s2_s.at[u], s2_r.at[u], par)

        def out_copy(u, j, lo, w):
            start = j * CW + lo
            cols = pl.ds(start if isinstance(start, int) else pl.multiple_of(start, CW), w)
            return pltpu.make_async_copy(sbuf.at[j, c, :, pl.ds(lo, w)], out_h.at[0, :, cols], o_sem.at[u])

        def down(u, j, lo, w):
            slot = lax.rem(j, DS)
            lanes = pl.ds(lo, w)
            if lo == 0:
                d_load(j, slot).wait()
            if w == CW:
                pbuf[j] = dot(act[...], dbuf[slot]).astype(BF16).reshape(2, 2, BT, w)
            else:
                for r in range(2):
                    part = dot(act[pl.ds(r * 2 * BT, 2 * BT), :], dbuf[slot, :, lanes])
                    pbuf[j, r, :, :, lanes] = part.astype(BF16).reshape(2, BT, w)
            p2_send(u, j, lo, w).start()

        def chip_sum(u, j, lo, w):
            lanes = pl.ds(lo, w)
            p2_send(u, j, lo, w).wait_recv()
            sbuf[j, oc, :, lanes] = (pbuf[j, oc, k, :, lanes].astype(F32) + psib[j, oc, :, lanes].astype(F32)).astype(BF16)
            s2_send(u, j, lo, w).start()

        def finish(u, j, lo, w):
            lanes = pl.ds(lo, w)
            s2_send(u, j, lo, w).wait_recv()
            total = pbuf[j, c, k, :, lanes].astype(F32) + psib[j, c, :, lanes].astype(F32) + xs2[j, :, lanes].astype(F32)
            sbuf[j, c, :, lanes] = (xa[j, c, k, :, lanes].astype(F32) + total).astype(BF16)
            out_copy(u, j, lo, w).start()

        outs = [(u,) + OUTS[u] for u in range(NO)]

        @pl.loop(0, NC - 1)
        def _(j):
            down(j, j, 0, CW)

            @pl.when(j + DS < NC)
            def _():
                d_load(j + DS, lax.rem(j, DS)).start()

            @pl.when(j > 0)
            def _():
                chip_sum(j - 1, j - 1, 0, CW)

        down(*outs[NO - 2])
        chip_sum(*outs[NO - 3])
        down(*outs[NO - 1])
        chip_sum(*outs[NO - 2])
        for u in range(NO - 4):
            finish(*outs[u])
        chip_sum(*outs[NO - 1])
        for u in range(NO - 4, NO):
            finish(*outs[u])

        for u in range(NU):
            x1_send(*unit[u]).wait_send()
        for u in range(NO):
            p2_send(*outs[u]).wait_send()
            s2_send(*outs[u]).wait_send()
            out_copy(*outs[u]).wait()

    pl.run_scoped(mlp_half,
                  pltpu.VMEM((T, FF), F32), pltpu.VMEM((T, FF), F32), pltpu.VMEM((T, FF), BF16),
                  pltpu.VMEM((DS, FF, CW), BF16))


def solution(mesh):
    def local_layer(hidden, positions, gain_attn, w_q, b_q, w_k, b_k, w_v, b_v, w_o, gain_mlp, w_gate, w_up, w_down):
        half = HEAD_DIM // 2
        freq = ROPE_THETA ** (-np.arange(half) / half)
        freq = np.concatenate([freq, freq]).reshape(1, HEAD_DIM).astype(np.float32)
        dma = pltpu.SemaphoreType.DMA
        sems = [dma((7,)), dma((NC,)), dma((NC, 3)), dma, dma((GH, 2)), dma((DS,)), dma((NO + 2,)),
                dma((NC,)), dma((NC,)), dma((NC,)), dma((NC,)), dma((NC,)), dma((NC,)), dma((3,)), dma((3,))]
        sems += [dma((NU,)) for _ in range(6)] + [dma((NO,)) for _ in range(4)]
        vm = pltpu.VMEM
        out, kc, vc = pl.pallas_call(
            layer_kernel,
            out_shape=(jax.ShapeDtypeStruct((1, BT, D), BF16), jax.ShapeDtypeStruct((T, HEAD_DIM), BF16),
                       jax.ShapeDtypeStruct((T, HEAD_DIM), BF16)),
            in_specs=[pl.BlockSpec(memory_space=pl.ANY)] * 15,
            out_specs=(pl.BlockSpec(memory_space=pl.ANY),) * 3,
            scratch_shapes=[
                vm((NC, 2, 2, BT, CW), BF16), vm((2, 2, 8, 128), F32),
                vm((GH, HW, FF), BF16), vm((GH, HW, FF), BF16),
                vm((NC, 2, 2, BT, CW), BF16), vm((NC, 2, BT, CW), BF16), vm((NC, 2, BT, CW), BF16), vm((NC, 2, BT, CW), BF16),
                vm((T, QW), BF16), vm((T, CW), BF16), vm((T, 128), F32), vm((T, 1), F32),
                vm((T, 128), F32), vm((NC, BT, CW), BF16),
                vm((D,), BF16), vm((D,), BF16), vm((QW,), BF16), vm((HEAD_DIM,), BF16), vm((HEAD_DIM,), BF16),
                vm((1, T), jnp.int32), vm((1, HEAD_DIM), F32),
            ] + sems,
            compiler_params=pltpu.CompilerParams(collective_id=0, has_side_effects=True, vmem_limit_bytes=67043328),
            name='layer',
        )(hidden, positions, gain_attn, w_q, b_q, w_k, b_k, w_v,
          b_v, w_o, gain_mlp, w_gate, w_up, w_down, freq)
        shapes = (jax.ShapeDtypeStruct((1, BT, D), BF16), jax.ShapeDtypeStruct((T, HEAD_DIM), BF16), jax.ShapeDtypeStruct((T, HEAD_DIM), BF16))
        out, kc, vc = pl.pallas_call(
            result_kernel,
            out_shape=shapes,
            in_specs=[pl.BlockSpec(memory_space=pl.ANY)] * 3,
            out_specs=(pl.BlockSpec(memory_space=pl.ANY),) * 3,
            scratch_shapes=[vm((NC, BT, CW), BF16), vm((2, T, HEAD_DIM), BF16), dma((NC + 2,)), dma((NC + 2,))],
            name='results',
        )(out, kc, vc)
        return out, kc.reshape(1, T, 1, HEAD_DIM), vc.reshape(1, T, 1, HEAD_DIM)

    token_rows = P('dp', 'tp', None)
    col_split = P(None, 'tp')
    row_split = P('tp', None)
    vec_split = P('tp')
    replicated = P(None)
    cache_spec = P('dp', None, 'tp', None)
    in_specs = (token_rows, P('dp', None), replicated, col_split, vec_split, col_split, vec_split, col_split, vec_split, row_split, replicated, col_split, col_split, row_split)
    out_specs = (token_rows, cache_spec, cache_spec)
    return jax.shard_map(local_layer, mesh=mesh, in_specs=in_specs, out_specs=out_specs, check_vma=False)
```

time: 82.1 us -> 68.4 us (0.83)
  local copies, waits for them, and re-layouts: 8.63 us -> 0 us
  Pallas kernels: 71.7 us -> 67.4 us
    pallas_call x1, Pallas kernels: 71.7 us -> 65.5 us  [local_layer(): pl.pallas_call(layer_kernel, out_shape=(jax.ShapeDtypeStruct((1, BT, D),...]
    unnamed x3 -> x0, local copies, waits for them, and re-layouts: 4.76 us -> none
    reshape x3 -> x0, local copies, waits for them, and re-layouts: 3.87 us -> none  [the longest x1 1.3 us: local_layer(): gain_attn.reshape(1, D)]
    pallas_call x0 -> x1, Pallas kernels: none -> 1.89 us  [local_layer(): pl.pallas_call(result_kernel, out_shape=shapes, in_specs=[pl.BlockSpec(me...]
where the time goes in v2:
time: 68.4 us; the launch traced here: 68.2 us
  Pallas kernels  67.4 us (99%)
  between operations  0.8 us (1%)
    pallas_call x1, Pallas kernels, local_layer(): pl.pallas_call(layer_kernel, out_shape=(jax.ShapeDtypeStruct((1, BT, D),...  65.5 us
    pallas_call x1, Pallas kernels, local_layer(): pl.pallas_call(result_kernel, out_shape=shapes, in_specs=[pl.BlockSpec(me...  1.89 us

profile of v2, /device:TPU:0, one launch (start us, length us, event | category | flops | bytes accessed | tf_op | source)
XLA Modules:
  0.0 68.2 jit_solution(18289159720671885358)
XLA Ops:
  0.6 65.5 %layer.1 = (bf16[1,64,3584]{2,1,0:T(8,128)(2,1)}, bf16[256,128]{1,0:T(8,128)(2,1)}, bf16[256,128]{1,0:T(8,128)(2,1)}) custom-call(bf16[1,64,3584]{2,1,0:T(8,128)(2,1)} %x_h.1, s32[1,256]{1,0:T(1,128)} %pos_h.1, bf16[3584]{0:T(1024)(128)(2,1)} %g1_h.1, bf16[3584,896]{1,0:T(8,128)(2,1)} %wq_h.1, bf16[896]{0:T(1024)(128)(2,1)} %bq_h.1, bf16[3584,128]{1,0:T(8,128)(2,1)} %wk_h.1, ...), custom_call_target="tpu_custom_call" | custom-call | tf_op jit(solution)/shard_map/layer/pallas_call | solution.py:462
  66.2 1.9 %results.1 = (bf16[1,64,3584]{2,1,0:T(8,128)(2,1)}, bf16[256,128]{1,0:T(8,128)(2,1)}, bf16[256,128]{1,0:T(8,128)(2,1)}) custom-call(bf16[1,64,3584]{2,1,0:T(8,128)(2,1)} %get-tuple-element.9.out_i, bf16[256,128]{1,0:T(8,128)(2,1)} %get-tuple-element.10.kc_i, bf16[256,128]{1,0:T(8,128)(2,1)} %get-tuple-element.11.vc_i), custom_call_target="tpu_custom_call" | custom-call | tf_op jit(solution)/shard_map/results/pallas_call | solution.py:482

commit v3 on v2

--- a/solution.py
+++ b/solution.py
@@ -21,10 +21,9 @@
 TW = 256
 GH = 5
 DS = 3
+LATE = 3
 HW = CW // 2
-UNITS = tuple((j, 0, CW) for j in range(NC))
-NU = len(UNITS)
-OUTS = tuple((j, 0, CW) for j in range(NC - 1)) + ((NC - 1, 0, HW), (NC - 1, HW, HW))
+OUTS = ((0, 0, HW), (0, HW, HW)) + tuple((j, 0, CW) for j in range(1, NC - 1)) + ((NC - 1, 0, HW), (NC - 1, HW, HW))
 NO = len(OUTS)
 F32 = jnp.float32
 BF16 = jnp.bfloat16
@@ -46,27 +45,22 @@
     return ref[pl.ds(start, size)].astype(F32).reshape(1, size)
 
 
-def result_kernel(out_i, kc_i, vc_i, out_o, kc_o, vc_o, outb, kvb, i_sem, o_sem):
-    loads = [(out_i.at[0, :, pl.ds(j * CW, CW)], outb.at[j]) for j in range(NC)] + [(kc_i, kvb.at[0]), (vc_i, kvb.at[1])]
-    stores = [(outb.at[j], out_o.at[0, :, pl.ds(j * CW, CW)]) for j in range(NC)] + [(kvb.at[0], kc_o), (kvb.at[1], vc_o)]
-    loads = [pltpu.make_async_copy(s, d, i_sem.at[i]) for i, (s, d) in enumerate(loads)]
-    stores = [pltpu.make_async_copy(s, d, o_sem.at[i]) for i, (s, d) in enumerate(stores)]
-    for cp in loads:
-        cp.start()
-    for load, store in zip(loads, stores):
-        load.wait()
-        store.start()
-    for store in stores:
-        store.wait()
+def result_kernel(out_i, kc_i, vc_i, out_o, kc_o, vc_o, outb, kb, vb, i_sem, o_sem):
+    loads = [pltpu.make_async_copy(s, d, i_sem) for s, d in ((out_i, outb), (kc_i, kb), (vc_i, vb))]
+    stores = [pltpu.make_async_copy(s, d, o_sem) for s, d in ((outb, out_o), (kb, kc_o), (vb, vc_o))]
+    for cps in (loads, stores):
+        for cp in cps:
+            cp.start()
+        for cp in cps:
+            cp.wait()
 
 
 def layer_kernel(x_h, pos_h, g1_h, wq_h, bq_h, wk_h, bk_h, wv_h, bv_h, wo_h, g2_h, wg_h, wu_h, wd_h, freq_h,
                  out_h, kc_h, vc_h,
                  xa, sta, gbuf, ubuf, pbuf, psib, sbuf, xs, obuf, hbuf, cprev, ssum, alpha, xs2,
                  g1, g2, bq, bk, bv, pos, freq,
-                 sm_sem, x_sem, w_sem, wo_sem, g_sem, d_sem, o_sem,
-                 xp_s, xp_r, xb_s, xb_r, xf_s, xf_r, st_s, st_r,
-                 ps_s, ps_r, sx_s, sx_r, x1_s, x1_r, p2_s, p2_r, s2_s, s2_r):
+                 sm_sem, x_sem, w_sem, wo_sem, g_sem, d_sem, o_sem, sent_x, sent_p, sent_o,
+                 xp_r, xb_r, xf_r, st_r, ps_r, sx_r):
     tp = lax.axis_index('tp')
     c = lax.div(tp, 2)
     k = lax.rem(tp, 2)
@@ -80,27 +74,27 @@
                                             device_id={'tp': target}, device_id_type=MESH)
 
     def x_load(j):
-        return pltpu.make_async_copy(x_h.at[0, :, pl.ds(j * CW, CW)], xa.at[j, c, k], x_sem.at[j])
+        return pltpu.make_async_copy(x_h.at[0, :, pl.ds(j * CW, CW)], xa.at[j, c, k], x_sem.at[min(j, 1)])
 
     for j in range(NC):
         x_load(j).start()
     small = [(g1_h, g1), (g2_h, g2), (bq_h, bq), (bk_h, bk), (bv_h, bv), (pos_h, pos), (freq_h, freq)]
-    small_cp = [pltpu.make_async_copy(s, d, sm_sem.at[i]) for i, (s, d) in enumerate(small)]
+    small_cp = [pltpu.make_async_copy(s, d, sm_sem) for i, (s, d) in enumerate(small)]
     for cp in small_cp:
         cp.start()
 
     def g_loads(i):
         slot = lax.rem(i, GH)
         rows = pl.ds(pl.multiple_of(i * HW, HW), HW)
-        return (pltpu.make_async_copy(wg_h.at[rows], gbuf.at[slot], g_sem.at[slot, 0]),
-                pltpu.make_async_copy(wu_h.at[rows], ubuf.at[slot], g_sem.at[slot, 1]))
+        return (pltpu.make_async_copy(wg_h.at[rows], gbuf.at[slot], g_sem.at[slot]),
+                pltpu.make_async_copy(wu_h.at[rows], ubuf.at[slot], g_sem.at[slot]))
 
     def attention_half(wb, wob, qkv):
         def w_loads(j):
             rows = pl.ds(j * CW, CW)
-            return (pltpu.make_async_copy(wq_h.at[rows], wb.at[j, :, pl.ds(0, QW)], w_sem.at[j, 0]),
-                    pltpu.make_async_copy(wk_h.at[rows], wb.at[j, :, pl.ds(QW, HEAD_DIM)], w_sem.at[j, 1]),
-                    pltpu.make_async_copy(wv_h.at[rows], wb.at[j, :, pl.ds(QW + HEAD_DIM, HEAD_DIM)], w_sem.at[j, 2]))
+            return (pltpu.make_async_copy(wq_h.at[rows], wb.at[j, :, pl.ds(0, QW)], w_sem.at[j]),
+                    pltpu.make_async_copy(wk_h.at[rows], wb.at[j, :, pl.ds(QW, HEAD_DIM)], w_sem.at[j]),
+                    pltpu.make_async_copy(wv_h.at[rows], wb.at[j, :, pl.ds(QW + HEAD_DIM, HEAD_DIM)], w_sem.at[j]))
 
         for j in range(NC):
             for cp in w_loads(j):
@@ -117,38 +111,38 @@
         pl.semaphore_wait(barrier, 2)
 
         def x_to_par(j):
-            return remote(xa.at[j, c, k], xa.at[j, c, k], xp_s.at[j], xp_r.at[j], par)
+            return remote(xa.at[j, c, k], xa.at[j, c, k], sent_x, xp_r.at[j], par)
 
         def x_from_par(j):
-            return remote(xa.at[j, oc, k], xa.at[j, oc, k], xp_s.at[j], xp_r.at[j], par)
+            return remote(xa.at[j, oc, k], xa.at[j, oc, k], sent_x, xp_r.at[j], par)
 
         def x_to_sib(j):
-            return remote(xa.at[j, c, k], xa.at[j, c, k], xb_s.at[j], xb_r.at[j], sib)
+            return remote(xa.at[j, c, k], xa.at[j, c, k], sent_x, xb_r.at[j], sib)
 
         def x_from_sib(j):
-            return remote(xa.at[j, c, ok], xa.at[j, c, ok], xb_s.at[j], xb_r.at[j], sib)
+            return remote(xa.at[j, c, ok], xa.at[j, c, ok], sent_x, xb_r.at[j], sib)
 
         def x_forward(j):
-            return remote(xa.at[j, oc, k], xa.at[j, oc, k], xf_s.at[j], xf_r.at[j], sib)
+            return remote(xa.at[j, oc, k], xa.at[j, oc, k], sent_x, xf_r.at[j], sib)
 
         def x_forwarded(j):
-            return remote(xa.at[j, oc, ok], xa.at[j, oc, ok], xf_s.at[j], xf_r.at[j], sib)
+            return remote(xa.at[j, oc, ok], xa.at[j, oc, ok], sent_x, xf_r.at[j], sib)
 
         x_load(0).wait()
         x_to_par(0).start()
         x_to_sib(0).start()
+        for j in range(1, NC):
+            x_load(j).wait()
         square = jnp.zeros((BT, CW), F32)
         for j in range(NC):
-            if j:
-                x_load(j).wait()
             part = xa[j, c, k].astype(F32)
             square = square + part * part
         mean = jnp.sum(square, axis=-1, keepdims=True) / D
         inv = jnp.broadcast_to(lax.rsqrt(mean + NORM_EPS), (BT, 128))
         sta[c, k] = jnp.transpose(jnp.concatenate([inv, inv], axis=0))[:8]
-        st_par = remote(sta.at[c, k], sta.at[c, k], st_s.at[0], st_r.at[0], par)
+        st_par = remote(sta.at[c, k], sta.at[c, k], sent_x, st_r.at[0], par)
         st_par.start()
-        st_sib = remote(sta.at[c, k], sta.at[c, k], st_s.at[1], st_r.at[1], sib)
+        st_sib = remote(sta.at[c, k], sta.at[c, k], sent_x, st_r.at[1], sib)
         st_sib.start()
         for j in range(1, NC):
             x_to_par(j).start()
@@ -163,11 +157,11 @@
         lane = lax.broadcasted_iota(jnp.int32, (T, HEAD_DIM), 1)
         sine = jnp.where(lane < HEAD_DIM // 2, -sine, sine)
 
-        remote(sta.at[oc, k], sta.at[oc, k], st_s.at[0], st_r.at[0], par).wait_recv()
-        st_fwd = remote(sta.at[oc, k], sta.at[oc, k], st_s.at[2], st_r.at[2], sib)
+        remote(sta.at[oc, k], sta.at[oc, k], sent_x, st_r.at[0], par).wait_recv()
+        st_fwd = remote(sta.at[oc, k], sta.at[oc, k], sent_x, st_r.at[2], sib)
         st_fwd.start()
-        remote(sta.at[c, ok], sta.at[c, ok], st_s.at[1], st_r.at[1], sib).wait_recv()
-        remote(sta.at[oc, ok], sta.at[oc, ok], st_s.at[2], st_r.at[2], sib).wait_recv()
+        remote(sta.at[c, ok], sta.at[c, ok], sent_x, st_r.at[1], sib).wait_recv()
+        remote(sta.at[oc, ok], sta.at[oc, ok], sent_x, st_r.at[2], sib).wait_recv()
         for cc in range(2):
             for kk in range(2):
                 wide = jnp.broadcast_to(sta[cc, kk][0:1], (128, 128))
@@ -196,48 +190,50 @@
 
         project(NC - 1)
 
-        def rotate(u):
-            return u * cosine + pltpu.roll(u, HEAD_DIM // 2, 1) * sine
-
-        key = rotate(qkv[:, pl.ds(QW, HEAD_DIM)] + row(bk, 0, HEAD_DIM)).astype(BF16)
-        value = (qkv[:, pl.ds(QW + HEAD_DIM, HEAD_DIM)] + row(bv, 0, HEAD_DIM)).astype(BF16)
-        key_lanes, value_lanes = pl.ds(0, HEAD_DIM), pl.ds(HEAD_DIM, HEAD_DIM)
-        hbuf[:, key_lanes] = key
-        hbuf[:, value_lanes] = value
-        k_out = pltpu.make_async_copy(hbuf.at[:, key_lanes], kc_h, o_sem.at[NO])
-        v_out = pltpu.make_async_copy(hbuf.at[:, value_lanes], vc_h, o_sem.at[NO + 1])
-        k_out.start()
-        v_out.start()
+        def rotate(u, r):
+            rows = slice(r * 2 * BT, (r + 1) * 2 * BT)
+            return u * cosine[rows] + pltpu.roll(u, HEAD_DIM // 2, 1) * sine[rows]
+
         half = T // 2
         rows = HEADS * half
         row_i = lax.rem(lax.broadcasted_iota(jnp.int32, (rows, half), 0), half)
         causal = row_i >= lax.broadcasted_iota(jnp.int32, (rows, half), 1)
-        query = [rotate(qkv[:, pl.ds(h * HEAD_DIM, HEAD_DIM)] + row(bq, h * HEAD_DIM, HEAD_DIM)).astype(BF16)
-                 for h in range(HEADS)]
+        key_lanes, value_lanes = pl.ds(0, HEAD_DIM), pl.ds(HEAD_DIM, HEAD_DIM)
         for r in range(2):
             width = half * (r + 1)
-            stacked = jnp.concatenate([q[r * half:(r + 1) * half] for q in query], axis=0)
-            scores = lax.dot_general(stacked, key[:width], (((1,), (1,)), ((), ())),
+            part = pl.ds(r * half, half)
+            hbuf[part, key_lanes] = rotate(qkv[part, pl.ds(QW, HEAD_DIM)] + row(bk, 0, HEAD_DIM), r).astype(BF16)
+            hbuf[part, value_lanes] = (qkv[part, pl.ds(QW + HEAD_DIM, HEAD_DIM)] + row(bv, 0, HEAD_DIM)).astype(BF16)
+            stacked = jnp.concatenate([
+                rotate(qkv[part, pl.ds(h * HEAD_DIM, HEAD_DIM)] + row(bq, h * HEAD_DIM, HEAD_DIM), r).astype(BF16)
+                for h in range(HEADS)], axis=0)
+            scores = lax.dot_general(stacked, hbuf[pl.ds(0, width), key_lanes], (((1,), (1,)), ((), ())),
                                      preferred_element_type=F32) * (HEAD_DIM ** -0.5)
             last = jnp.where(causal, scores[:, width - half:], -1e30)
             scores = last if r == 0 else jnp.concatenate([scores[:, :half], last], axis=1)
             weights = jnp.exp(scores - jnp.max(scores, axis=-1, keepdims=True))
             probs = (weights * (1.0 / jnp.sum(weights, axis=-1, keepdims=True))).astype(BF16)
-            out = dot(probs, value[:width]).astype(BF16)
+            out = dot(probs, hbuf[pl.ds(0, width), value_lanes]).astype(BF16)
             for h in range(HEADS):
-                obuf[pl.ds(r * half, half), pl.ds(h * HEAD_DIM, HEAD_DIM)] = out[h * half:(h + 1) * half]
-
-        wo_cp.wait()
-
+                obuf[part, pl.ds(h * HEAD_DIM, HEAD_DIM)] = out[h * half:(h + 1) * half]
+            if r == 0:
+                wo_cp.wait()
+            pbuf[0, r] = dot(obuf[part, :], wob[:, pl.ds(0, CW)]).astype(BF16).reshape(2, BT, CW)
+            p_sends(0)[r].start()
+
+        k_out = pltpu.make_async_copy(hbuf.at[:, key_lanes], kc_h, o_sem)
+        v_out = pltpu.make_async_copy(hbuf.at[:, value_lanes], vc_h, o_sem)
+        k_out.start()
+        v_out.start()
+        chip_partial(0, 0)
         lag = 3
-        for u, (j, lo, w) in enumerate(UNITS):
-            part = dot(obuf[...], wob[:, pl.ds(j * CW + lo, w)]).astype(BF16)
-            pbuf[j, :, :, :, pl.ds(lo, w)] = part.reshape(2, 2, BT, w)
-            p_send(u, j, lo, w).start()
-            if u >= lag:
-                chip_partial(u - lag)
-        for u in range(NU - lag, NU):
-            chip_partial(u)
+        for j in range(1, NC):
+            pbuf[j] = dot(obuf[...], wob[:, pl.ds(j * CW, CW)]).astype(BF16).reshape(2, 2, BT, CW)
+            p_sends(j)[0].start()
+            if j >= lag:
+                chip_partial(j - lag, 1 if j == lag else 0)
+        for j in range(NC - lag, NC):
+            chip_partial(j, 0)
 
         @pl.loop(0, NC)
         def _(j):
@@ -251,20 +247,22 @@
         k_out.wait()
         v_out.wait()
 
-    def p_send(u, j, lo, w):
-        lanes = pl.ds(lo, w)
-        return remote(pbuf.at[j, :, ok, :, lanes], psib.at[j, :, :, lanes], ps_s.at[u], ps_r.at[u], sib)
-
-    def s_send(u, j, lo, w):
-        lanes = pl.ds(lo, w)
-        return remote(sbuf.at[j, :, :, lanes], xs.at[j, :, :, lanes], sx_s.at[u], sx_r.at[u], par)
-
-    def chip_partial(u):
-        j, lo, w = UNITS[u]
-        lanes = pl.ds(lo, w)
-        p_send(u, j, lo, w).wait_recv()
-        sbuf[j, :, :, lanes] = (pbuf[j, :, k, :, lanes].astype(F32) + psib[j, :, :, lanes].astype(F32)).astype(BF16)
-        s_send(u, j, lo, w).start()
+    def parts(j):
+        if isinstance(j, int) and j == 0:
+            return ((pl.ds(0, 1), 0), (pl.ds(1, 1), NC))
+        return ((pl.ds(0, 2), j),)
+
+    def p_sends(j):
+        return [remote(pbuf.at[j, p, ok], psib.at[j, p], sent_p, ps_r.at[i], sib) for p, i in parts(j)]
+
+    def s_sends(j):
+        return [remote(sbuf.at[j, p], xs.at[j, p], sent_p, sx_r.at[i], par) for p, i in parts(j)]
+
+    def chip_partial(j, which):
+        p = parts(j)[which][0]
+        p_sends(j)[which].wait_recv()
+        sbuf[j, p] = (pbuf[j, p, k].astype(F32) + psib[j, p].astype(F32)).astype(BF16)
+        s_sends(j)[which].start()
 
     pl.run_scoped(attention_half,
                   pltpu.VMEM((NC, CW, QKV), BF16), pltpu.VMEM((QW, D), BF16), pltpu.VMEM((T, QKV), F32))
@@ -277,20 +275,18 @@
         for s in range(DS):
             d_load(s, s).start()
 
-        def x1_send(u, j, lo, w):
-            part = xa.at[j, :, k, :, pl.ds(lo, w)]
-            return remote(part, part, x1_s.at[u], x1_r.at[u], sib)
-
-        def x1_recv(u, j, lo, w):
-            part = xa.at[j, :, ok, :, pl.ds(lo, w)]
-            return remote(part, part, x1_s.at[u], x1_r.at[u], sib)
-
-        def residual(u, j, lo, w):
-            lanes = pl.ds(lo, w)
-            s_send(u, j, lo, w).wait_recv()
-            total = sbuf[j, :, :, lanes].astype(F32) + xs[j, :, :, lanes].astype(F32)
-            xa[j, :, k, :, lanes] = (xa[j, :, k, :, lanes].astype(F32) + total).astype(BF16)
-            x1_send(u, j, lo, w).start()
+        def x1_send(j):
+            return remote(xa.at[j, :, k], xa.at[j, :, k], sent_o, xb_r.at[j], sib)
+
+        def x1_recv(j):
+            return remote(xa.at[j, :, ok], xa.at[j, :, ok], sent_o, xb_r.at[j], sib)
+
+        def residual(j):
+            for cp in s_sends(j):
+                cp.wait_recv()
+            total = sbuf[j].astype(F32) + xs[j].astype(F32)
+            xa[j, :, k] = (xa[j, :, k].astype(F32) + total).astype(BF16)
+            x1_send(j).start()
 
         def normalise(u):
             values = xa[u].reshape(T, CW).astype(F32)
@@ -336,17 +332,20 @@
         NT = FF // TW
 
         def gate_up(u, mode, cut):
-            x1_recv(u, u, 0, CW).wait_recv()
+            x1_recv(u).wait_recv()
             for i in range(2):
                 for cp in g_loads(2 * u + i):
                     cp.wait()
             halves = [lax.rem(2 * u + i, GH) for i in range(2)]
+            if cut == 0:
+                residual(u + 1)
             normalise(u)
             if mode == 'last':
                 tiles(halves, mode, 0, NT)
             else:
                 tiles(halves, mode, 0, cut)
-                residual(u + 1, u + 1, 0, CW)
+                if cut:
+                    residual(u + 1)
                 tiles(halves, mode, cut, NT)
             tail(halves, mode)
 
@@ -354,38 +353,38 @@
             for cp in g_loads(i):
                 cp.start()
 
-        unit = [(u,) + UNITS[u] for u in range(NU)]
-        residual(*unit[0])
+        residual(0)
         gate_up(0, 'first', 13)
         for i in range(2):
             refill(GH + i)
 
-        @pl.loop(1, NC - 1)
-        def _(u):
-            gate_up(u, 'mid', 9)
+        def middle(u, cut):
+            gate_up(u, 'mid', cut)
             for i in range(2):
                 @pl.when(2 * u + i + GH < 2 * NC)
                 def _():
                     refill(2 * u + i + GH)
 
+        pl.loop(1, LATE)(lambda u: middle(u, 9))
+        pl.loop(LATE, NC - 1)(lambda u: middle(u, 0))
         gate_up(NC - 1, 'last', NT)
 
-        for u in range(NU):
-            p_send(*unit[u]).wait_send()
-            s_send(*unit[u]).wait_send()
+        for j in range(NC):
+            for cp in p_sends(j) + s_sends(j):
+                cp.wait_send()
 
         def p2_send(u, j, lo, w):
             lanes = pl.ds(lo, w)
-            return remote(pbuf.at[j, :, ok, :, lanes], psib.at[j, :, :, lanes], p2_s.at[u], p2_r.at[u], sib)
+            return remote(pbuf.at[j, :, ok, :, lanes], psib.at[j, :, :, lanes], sent_o, ps_r.at[u], sib)
 
         def s2_send(u, j, lo, w):
             lanes = pl.ds(lo, w)
-            return remote(sbuf.at[j, oc, :, lanes], xs2.at[j, :, lanes], s2_s.at[u], s2_r.at[u], par)
+            return remote(sbuf.at[j, oc, :, lanes], xs2.at[j, :, lanes], sent_o, xp_r.at[u], par)
 
         def out_copy(u, j, lo, w):
             start = j * CW + lo
             cols = pl.ds(start if isinstance(start, int) else pl.multiple_of(start, CW), w)
-            return pltpu.make_async_copy(sbuf.at[j, c, :, pl.ds(lo, w)], out_h.at[0, :, cols], o_sem.at[u])
+            return pltpu.make_async_copy(sbuf.at[j, c, :, pl.ds(lo, w)], out_h.at[0, :, cols], o_sem)
 
         def down(u, j, lo, w):
             slot = lax.rem(j, DS)
@@ -415,17 +414,26 @@
 
         outs = [(u,) + OUTS[u] for u in range(NO)]
 
-        @pl.loop(0, NC - 1)
+        down(*outs[0])
+        down(*outs[1])
+        d_load(DS, 0).start()
+        chip_sum(*outs[0])
+
+        @pl.loop(1, NC - 1)
         def _(j):
-            down(j, j, 0, CW)
+            down(j + 1, j, 0, CW)
 
             @pl.when(j + DS < NC)
             def _():
                 d_load(j + DS, lax.rem(j, DS)).start()
 
-            @pl.when(j > 0)
+            @pl.when(j == 1)
             def _():
-                chip_sum(j - 1, j - 1, 0, CW)
+                chip_sum(*outs[1])
+
+            @pl.when(j > 1)
+            def _():
+                chip_sum(j, j - 1, 0, CW)
 
         down(*outs[NO - 2])
         chip_sum(*outs[NO - 3])
@@ -437,8 +445,8 @@
         for u in range(NO - 4, NO):
             finish(*outs[u])
 
-        for u in range(NU):
-            x1_send(*unit[u]).wait_send()
+        for j in range(NC):
+            x1_send(j).wait_send()
         for u in range(NO):
             p2_send(*outs[u]).wait_send()
             s2_send(*outs[u]).wait_send()
@@ -455,9 +463,8 @@
         freq = ROPE_THETA ** (-np.arange(half) / half)
         freq = np.concatenate([freq, freq]).reshape(1, HEAD_DIM).astype(np.float32)
         dma = pltpu.SemaphoreType.DMA
-        sems = [dma((7,)), dma((NC,)), dma((NC, 3)), dma, dma((GH, 2)), dma((DS,)), dma((NO + 2,)),
-                dma((NC,)), dma((NC,)), dma((NC,)), dma((NC,)), dma((NC,)), dma((NC,)), dma((3,)), dma((3,))]
-        sems += [dma((NU,)) for _ in range(6)] + [dma((NO,)) for _ in range(4)]
+        sems = [dma, dma((2,)), dma((NC,)), dma, dma((GH,)), dma((DS,)), dma, dma, dma, dma,
+                dma((NO,)), dma((NC,)), dma((NC,)), dma((3,)), dma((NO,)), dma((NC + 1,))]
         vm = pltpu.VMEM
         out, kc, vc = pl.pallas_call(
             layer_kernel,
@@ -484,7 +491,7 @@
             out_shape=shapes,
             in_specs=[pl.BlockSpec(memory_space=pl.ANY)] * 3,
             out_specs=(pl.BlockSpec(memory_space=pl.ANY),) * 3,
-            scratch_shapes=[vm((NC, BT, CW), BF16), vm((2, T, HEAD_DIM), BF16), dma((NC + 2,)), dma((NC + 2,))],
+            scratch_shapes=[vm((1, BT, D), BF16), vm((T, HEAD_DIM), BF16), vm((T, HEAD_DIM), BF16), dma, dma],
             name='results',
         )(out, kc, vc)
         return out, kc.reshape(1, T, 1, HEAD_DIM), vc.reshape(1, T, 1, HEAD_DIM)

time: 68.4 us -> 66.5 us (0.972)
  Pallas kernels: 67.4 us -> 65.6 us
    pallas_call x1, Pallas kernels: 65.5 us -> 63.7 us  [local_layer(): pl.pallas_call(layer_kernel, out_shape=(jax.ShapeDtypeStruct((1, BT, D),...]
where the time goes in v3:
time: 66.5 us; the launch traced here: 66.4 us
  Pallas kernels  65.6 us (99%)
  between operations  0.8 us (1%)
    pallas_call x1, Pallas kernels, local_layer(): pl.pallas_call(layer_kernel, out_shape=(jax.ShapeDtypeStruct((1, BT, D),...  63.7 us
    pallas_call x1, Pallas kernels, local_layer(): pl.pallas_call(result_kernel, out_shape=shapes, in_specs=[pl.BlockSpec(me...  1.84 us

profile of v3, /device:TPU:0, one launch (start us, length us, event | category | flops | bytes accessed | tf_op | source)
XLA Modules:
  0.0 66.4 jit_solution(498552128774284449)
XLA Ops:
  0.6 63.7 %layer.1 = (bf16[1,64,3584]{2,1,0:T(8,128)(2,1)}, bf16[256,128]{1,0:T(8,128)(2,1)}, bf16[256,128]{1,0:T(8,128)(2,1)}) custom-call(bf16[1,64,3584]{2,1,0:T(8,128)(2,1)} %x_h.1, s32[1,256]{1,0:T(1,128)} %pos_h.1, bf16[3584]{0:T(1024)(128)(2,1)} %g1_h.1, bf16[3584,896]{1,0:T(8,128)(2,1)} %wq_h.1, bf16[896]{0:T(1024)(128)(2,1)} %bq_h.1, bf16[3584,128]{1,0:T(8,128)(2,1)} %wk_h.1, ...), custom_call_target="tpu_custom_call" | custom-call | tf_op jit(solution)/shard_map/layer/pallas_call | solution.py:469
  64.4 1.8 %results.1 = (bf16[1,64,3584]{2,1,0:T(8,128)(2,1)}, bf16[256,128]{1,0:T(8,128)(2,1)}, bf16[256,128]{1,0:T(8,128)(2,1)}) custom-call(bf16[1,64,3584]{2,1,0:T(8,128)(2,1)} %get-tuple-element.9.out_i, bf16[256,128]{1,0:T(8,128)(2,1)} %get-tuple-element.10.kc_i, bf16[256,128]{1,0:T(8,128)(2,1)} %get-tuple-element.11.vc_i), custom_call_target="tpu_custom_call" | custom-call | tf_op jit(solution)/shard_map/results/pallas_call | solution.py:489

commit v4 on v3

--- a/solution.py
+++ b/solution.py
@@ -23,8 +23,8 @@
 DS = 3
 LATE = 3
 HW = CW // 2
-OUTS = ((0, 0, HW), (0, HW, HW)) + tuple((j, 0, CW) for j in range(1, NC - 1)) + ((NC - 1, 0, HW), (NC - 1, HW, HW))
-NO = len(OUTS)
+NO = NC + 2
+SPLIT = NC - 2
 F32 = jnp.float32
 BF16 = jnp.bfloat16
 MESH = pl.DeviceIdType.MESH
@@ -195,7 +195,7 @@
             return u * cosine[rows] + pltpu.roll(u, HEAD_DIM // 2, 1) * sine[rows]
 
         half = T // 2
-        rows = HEADS * half
+        rows = 4 * half
         row_i = lax.rem(lax.broadcasted_iota(jnp.int32, (rows, half), 0), half)
         causal = row_i >= lax.broadcasted_iota(jnp.int32, (rows, half), 1)
         key_lanes, value_lanes = pl.ds(0, HEAD_DIM), pl.ds(HEAD_DIM, HEAD_DIM)
@@ -204,18 +204,19 @@
             part = pl.ds(r * half, half)
             hbuf[part, key_lanes] = rotate(qkv[part, pl.ds(QW, HEAD_DIM)] + row(bk, 0, HEAD_DIM), r).astype(BF16)
             hbuf[part, value_lanes] = (qkv[part, pl.ds(QW + HEAD_DIM, HEAD_DIM)] + row(bv, 0, HEAD_DIM)).astype(BF16)
-            stacked = jnp.concatenate([
-                rotate(qkv[part, pl.ds(h * HEAD_DIM, HEAD_DIM)] + row(bq, h * HEAD_DIM, HEAD_DIM), r).astype(BF16)
-                for h in range(HEADS)], axis=0)
-            scores = lax.dot_general(stacked, hbuf[pl.ds(0, width), key_lanes], (((1,), (1,)), ((), ())),
-                                     preferred_element_type=F32) * (HEAD_DIM ** -0.5)
-            last = jnp.where(causal, scores[:, width - half:], -1e30)
-            scores = last if r == 0 else jnp.concatenate([scores[:, :half], last], axis=1)
-            weights = jnp.exp(scores - jnp.max(scores, axis=-1, keepdims=True))
-            probs = (weights * (1.0 / jnp.sum(weights, axis=-1, keepdims=True))).astype(BF16)
-            out = dot(probs, hbuf[pl.ds(0, width), value_lanes]).astype(BF16)
-            for h in range(HEADS):
-                obuf[part, pl.ds(h * HEAD_DIM, HEAD_DIM)] = out[h * half:(h + 1) * half]
+            for heads in (range(4), range(4, HEADS)):
+                stacked = jnp.concatenate([
+                    rotate(qkv[part, pl.ds(h * HEAD_DIM, HEAD_DIM)] + row(bq, h * HEAD_DIM, HEAD_DIM), r).astype(BF16)
+                    for h in heads], axis=0)
+                scores = lax.dot_general(stacked, hbuf[pl.ds(0, width), key_lanes], (((1,), (1,)), ((), ())),
+                                         preferred_element_type=F32) * (HEAD_DIM ** -0.5)
+                last = jnp.where(causal[:len(heads) * half], scores[:, width - half:], -1e30)
+                scores = last if r == 0 else jnp.concatenate([scores[:, :half], last], axis=1)
+                weights = jnp.exp(scores - jnp.max(scores, axis=-1, keepdims=True))
+                probs = (weights * (1.0 / jnp.sum(weights, axis=-1, keepdims=True))).astype(BF16)
+                out = dot(probs, hbuf[pl.ds(0, width), value_lanes]).astype(BF16)
+                for i, h in enumerate(heads):
+                    obuf[part, pl.ds(h * HEAD_DIM, HEAD_DIM)] = out[i * half:(i + 1) * half]
             if r == 0:
                 wo_cp.wait()
             pbuf[0, r] = dot(obuf[part, :], wob[:, pl.ds(0, CW)]).astype(BF16).reshape(2, BT, CW)
@@ -373,84 +374,74 @@
             for cp in p_sends(j) + s_sends(j):
                 cp.wait_send()
 
-        def p2_send(u, j, lo, w):
-            lanes = pl.ds(lo, w)
-            return remote(pbuf.at[j, :, ok, :, lanes], psib.at[j, :, :, lanes], sent_o, ps_r.at[u], sib)
-
-        def s2_send(u, j, lo, w):
-            lanes = pl.ds(lo, w)
-            return remote(sbuf.at[j, oc, :, lanes], xs2.at[j, :, lanes], sent_o, xp_r.at[u], par)
-
-        def out_copy(u, j, lo, w):
-            start = j * CW + lo
-            cols = pl.ds(start if isinstance(start, int) else pl.multiple_of(start, CW), w)
-            return pltpu.make_async_copy(sbuf.at[j, c, :, pl.ds(lo, w)], out_h.at[0, :, cols], o_sem)
-
-        def down(u, j, lo, w):
+        def p2_send(j):
+            return remote(pbuf.at[j, :, ok], psib.at[j], sent_o, ps_r.at[j], sib)
+
+        def p2_block(j, block, sem):
+            return remote(pbuf.at[j, block, ok], psib.at[j, block], sent_o, ps_r.at[sem], sib)
+
+        def s2_send(j):
+            return remote(sbuf.at[j, oc], xs2.at[j], sent_o, xp_r.at[j], par)
+
+        def out_copy(j):
+            return pltpu.make_async_copy(sbuf.at[j, c], out_h.at[0, :, pl.ds(pl.multiple_of(j * CW, CW), CW)], o_sem)
+
+        def down(j):
             slot = lax.rem(j, DS)
-            lanes = pl.ds(lo, w)
-            if lo == 0:
-                d_load(j, slot).wait()
-            if w == CW:
-                pbuf[j] = dot(act[...], dbuf[slot]).astype(BF16).reshape(2, 2, BT, w)
-            else:
-                for r in range(2):
-                    part = dot(act[pl.ds(r * 2 * BT, 2 * BT), :], dbuf[slot, :, lanes])
-                    pbuf[j, r, :, :, lanes] = part.astype(BF16).reshape(2, BT, w)
-            p2_send(u, j, lo, w).start()
-
-        def chip_sum(u, j, lo, w):
-            lanes = pl.ds(lo, w)
-            p2_send(u, j, lo, w).wait_recv()
-            sbuf[j, oc, :, lanes] = (pbuf[j, oc, k, :, lanes].astype(F32) + psib[j, oc, :, lanes].astype(F32)).astype(BF16)
-            s2_send(u, j, lo, w).start()
-
-        def finish(u, j, lo, w):
-            lanes = pl.ds(lo, w)
-            s2_send(u, j, lo, w).wait_recv()
-            total = pbuf[j, c, k, :, lanes].astype(F32) + psib[j, c, :, lanes].astype(F32) + xs2[j, :, lanes].astype(F32)
-            sbuf[j, c, :, lanes] = (xa[j, c, k, :, lanes].astype(F32) + total).astype(BF16)
-            out_copy(u, j, lo, w).start()
-
-        outs = [(u,) + OUTS[u] for u in range(NO)]
-
-        down(*outs[0])
-        down(*outs[1])
+            d_load(j, slot).wait()
+            pbuf[j] = dot(act[...], dbuf[slot]).astype(BF16).reshape(2, 2, BT, CW)
+            p2_send(j).start()
+
+        def down_rows(j, block, sem):
+            rows = pl.ds(pl.multiple_of(block * 2 * BT, 2 * BT), 2 * BT)
+            pbuf[j, block] = dot(act[rows, :], dbuf[j % DS]).astype(BF16).reshape(2, BT, CW)
+            p2_block(j, block, sem).start()
+
+        def chip_sum(j, recv):
+            recv.wait_recv()
+            sbuf[j, oc] = (pbuf[j, oc, k].astype(F32) + psib[j, oc].astype(F32)).astype(BF16)
+            s2_send(j).start()
+
+        def finish(j):
+            s2_send(j).wait_recv()
+            total = pbuf[j, c, k].astype(F32) + psib[j, c].astype(F32) + xs2[j].astype(F32)
+            sbuf[j, c] = (xa[j, c, k].astype(F32) + total).astype(BF16)
+            out_copy(j).start()
+
+        down(0)
         d_load(DS, 0).start()
-        chip_sum(*outs[0])
-
-        @pl.loop(1, NC - 1)
+
+        @pl.loop(1, SPLIT)
         def _(j):
-            down(j + 1, j, 0, CW)
+            down(j)
 
             @pl.when(j + DS < NC)
             def _():
                 d_load(j + DS, lax.rem(j, DS)).start()
 
-            @pl.when(j == 1)
-            def _():
-                chip_sum(*outs[1])
-
-            @pl.when(j > 1)
-            def _():
-                chip_sum(j, j - 1, 0, CW)
-
-        down(*outs[NO - 2])
-        chip_sum(*outs[NO - 3])
-        down(*outs[NO - 1])
-        chip_sum(*outs[NO - 2])
-        for u in range(NO - 4):
-            finish(*outs[u])
-        chip_sum(*outs[NO - 1])
-        for u in range(NO - 4, NO):
-            finish(*outs[u])
+            chip_sum(j - 1, p2_send(j - 1))
+
+        one, two = SPLIT, SPLIT + 1
+        d_load(one, one % DS).wait()
+        down_rows(one, oc, one)
+        chip_sum(one - 1, p2_send(one - 1))
+        d_load(two, two % DS).wait()
+        down_rows(two, oc, two)
+        chip_sum(one, p2_block(one, oc, one))
+        down_rows(one, c, NC)
+        chip_sum(two, p2_block(two, oc, two))
+        down_rows(two, c, NC + 1)
+        pl.loop(0, SPLIT)(finish)
+        p2_block(one, c, NC).wait_recv()
+        finish(one)
+        p2_block(two, c, NC + 1).wait_recv()
+        finish(two)
 
         for j in range(NC):
             x1_send(j).wait_send()
-        for u in range(NO):
-            p2_send(*outs[u]).wait_send()
-            s2_send(*outs[u]).wait_send()
-            out_copy(*outs[u]).wait()
+            p2_send(j).wait_send()
+            s2_send(j).wait_send()
+            out_copy(j).wait()
 
     pl.run_scoped(mlp_half,
                   pltpu.VMEM((T, FF), F32), pltpu.VMEM((T, FF), F32), pltpu.VMEM((T, FF), BF16),

time: 66.5 us -> 65.8 us (0.989)
  Pallas kernels: 65.6 us -> 64.9 us
    pallas_call x1, Pallas kernels: 63.7 us -> 63 us  [local_layer(): pl.pallas_call(layer_kernel, out_shape=(jax.ShapeDtypeStruct((1, BT, D),...]
where the time goes in v4:
time: 65.8 us; the launch traced here: 65.7 us
  Pallas kernels  64.9 us (99%)
  between operations  0.8 us (1%)
    pallas_call x1, Pallas kernels, local_layer(): pl.pallas_call(layer_kernel, out_shape=(jax.ShapeDtypeStruct((1, BT, D),...  63 us
    pallas_call x1, Pallas kernels, local_layer(): pl.pallas_call(result_kernel, out_shape=shapes, in_specs=[pl.BlockSpec(me...  1.84 us

profile of v4, /device:TPU:0, one launch (start us, length us, event | category | flops | bytes accessed | tf_op | source)
XLA Modules:
  0.0 65.7 jit_solution(5830228220675080889)
XLA Ops:
  0.6 63.0 %layer.1 = (bf16[1,64,3584]{2,1,0:T(8,128)(2,1)}, bf16[256,128]{1,0:T(8,128)(2,1)}, bf16[256,128]{1,0:T(8,128)(2,1)}) custom-call(bf16[1,64,3584]{2,1,0:T(8,128)(2,1)} %x_h.1, s32[1,256]{1,0:T(1,128)} %pos_h.1, bf16[3584]{0:T(1024)(128)(2,1)} %g1_h.1, bf16[3584,896]{1,0:T(8,128)(2,1)} %wq_h.1, bf16[896]{0:T(1024)(128)(2,1)} %bq_h.1, bf16[3584,128]{1,0:T(8,128)(2,1)} %wk_h.1, ...), custom_call_target="tpu_custom_call" | custom-call | tf_op jit(solution)/shard_map/layer/pallas_call | solution.py:460
  63.7 1.8 %results.1 = (bf16[1,64,3584]{2,1,0:T(8,128)(2,1)}, bf16[256,128]{1,0:T(8,128)(2,1)}, bf16[256,128]{1,0:T(8,128)(2,1)}) custom-call(bf16[1,64,3584]{2,1,0:T(8,128)(2,1)} %get-tuple-element.9.out_i, bf16[256,128]{1,0:T(8,128)(2,1)} %get-tuple-element.10.kc_i, bf16[256,128]{1,0:T(8,128)(2,1)} %get-tuple-element.11.vc_i), custom_call_target="tpu_custom_call" | custom-call | tf_op jit(solution)/shard_map/results/pallas_call | solution.py:480
